TPU v7x, 32 devices: a whole 2x2x4 slice. The times are simulated.
32 devices in a mesh: dp: 2 (over x), tp: 4 (over z), sp: 4 (over y, core).
Axes of the slice: x: 2, y: 2, z: 4, core: 2. Of those that a mesh axis runs over, the one named last changes fastest.
Arguments:
- step_emb: bfloat16 [4, 4, 768], P(None, 'dp'), parts along dimension 1
- v_cache: bfloat16 [2, 4, 16384, 768], P(None, 'dp', 'sp', 'tp'), parts along dimension 1
- z_cache: bfloat16 [2, 4, 16384, 768], P(None, 'dp', 'sp', 'tp'), parts along dimension 1
- short_state: bfloat16 [2, 4, 2, 3, 768], P(None, 'dp', None, None, 'tp'), parts along dimension 1
- w_in: bfloat16 [2, 768, 3, 768], P(None, None, None, 'tp')
- b_in: float32 [2, 3, 768], P(None, None, 'tp')
- short_taps: float32 [2, 3, 3, 768], P(None, None, None, 'tp')
- long_filt: float32 [2, 2, 16384, 768], P(None, None, None, 'tp')
- skip_gain: float32 [2, 2, 768], P(None, None, 'tp')
- w_out: bfloat16 [2, 768, 768], P(None, 'tp')
- b_out: float32 [2, 768], replicated
- w_up: bfloat16 [2, 768, 3072], P(None, None, 'tp')
- w_down: bfloat16 [2, 3072, 768], P(None, 'tp')
Outputs:
- output 1: float32 [4, 4, 768], P(None, 'dp'), parts along dimension 1
- output 2: bfloat16 [2, 4, 16384, 768], P(None, 'dp', 'sp', 'tp'), parts along dimension 1
- output 3: bfloat16 [2, 4, 16384, 768], P(None, 'dp', 'sp', 'tp'), parts along dimension 1
- output 4: bfloat16 [2, 4, 2, 3, 768], P(None, 'dp', None, None, 'tp'), parts along dimension 1
There are 2 independent parts. A program takes and returns all parts, laid end to end along the dimension named above; an argument that names none is the same for every part.
All inputs are finite; a program needn't handle non-finite values.
Results may differ from a plain program's by a relative error of at most 0.010954.
Values sent between devices are 32-bit elements.
A program may use at most 1 GiB of HBM per device.

v0:
```python
import jax
import jax.numpy as jnp
from jax import lax
from jax.sharding import PartitionSpec as P

NUM_STEPS = 4
NUM_LAYERS = 2


def layer_norm(rows_in):
    mean_val = jnp.mean(rows_in, axis=-1, keepdims=True)
    centered = rows_in - mean_val
    var_val = jnp.mean(centered * centered, axis=-1, keepdims=True)
    return centered * lax.rsqrt(var_val + 1e-5)


def filter_windows(long_filt, shard_start, start_pos, shard_len):
    lag_pos = start_pos + 3 - shard_start - jnp.arange(shard_len + 3)
    picked = jnp.take(long_filt, jnp.maximum(lag_pos, 0), axis=2)
    return jnp.where((lag_pos >= 0)[:, None], picked, 0.0)


def append_row(cache_all, layer_idx, new_row, local_pos):
    num_seq = cache_all.shape[1]
    shard_len = cache_all.shape[2]
    chan_dim = cache_all.shape[3]
    inside = (local_pos >= 0) & (local_pos < shard_len)
    row_slot = jnp.clip(local_pos, 0, shard_len - 1)
    old_row = lax.dynamic_slice(cache_all, (layer_idx, 0, row_slot, 0), (1, num_seq, 1, chan_dim))
    put_row = jnp.where(inside, new_row[None, :, None, :], old_row)
    return lax.dynamic_update_slice(cache_all, put_row, (layer_idx, 0, row_slot, 0))


def solution(mesh):
    sp_size = mesh.shape["sp"]

    def device_fn(step_emb, v_cache, z_cache, short_state, w_in, b_in, short_taps, long_filt, skip_gain, w_out, b_out, w_up, w_down):
        shard_len = v_cache.shape[2]
        start_pos = shard_len * sp_size * 3 // 4
        shard_start = lax.axis_index("sp") * shard_len
        windows = filter_windows(long_filt, shard_start, start_pos, shard_len)
        v_all = v_cache
        z_all = z_cache
        states = [short_state[layer_idx] for layer_idx in range(NUM_LAYERS)]
        hidden_rows = []
        for step_idx in range(NUM_STEPS):
            local_pos = start_pos + step_idx - shard_start
            win_start = 3 - step_idx
            hidden = step_emb[step_idx].astype(jnp.float32)
            for layer_idx in range(NUM_LAYERS):
                normed = layer_norm(hidden).astype(jnp.bfloat16)
                proj_row = jnp.einsum("bd,dgc->bgc", normed, w_in[layer_idx], preferred_element_type=jnp.float32)
                proj_row = (proj_row + b_in[layer_idx]).astype(jnp.bfloat16)
                prev_state = states[layer_idx]
                tap_rows = short_taps[layer_idx]
                mixed_rows = (tap_rows[0] * proj_row.astype(jnp.float32)
                              + tap_rows[1] * prev_state[:, 1].astype(jnp.float32)
                              + tap_rows[2] * prev_state[:, 0].astype(jnp.float32))
                states[layer_idx] = jnp.stack([prev_state[:, 1], proj_row], axis=1)
                value_row = mixed_rows[:, 2].astype(jnp.bfloat16)
                v_all = append_row(v_all, layer_idx, value_row, local_pos)
                part_one = jnp.sum(v_all[layer_idx] * windows[layer_idx, 0, win_start:win_start + shard_len][None], axis=1)
                long_one = lax.psum(part_one, "sp") + skip_gain[layer_idx, 0] * value_row.astype(jnp.float32)
                z_row = (mixed_rows[:, 0] * long_one).astype(jnp.bfloat16)
                z_all = append_row(z_all, layer_idx, z_row, local_pos)
                part_two = jnp.sum(z_all[layer_idx] * windows[layer_idx, 1, win_start:win_start + shard_len][None], axis=1)
                long_two = lax.psum(part_two, "sp") + skip_gain[layer_idx, 1] * z_row.astype(jnp.float32)
                y_row = (mixed_rows[:, 1] * long_two).astype(jnp.bfloat16)
                mix_out = lax.psum(jnp.dot(y_row, w_out[layer_idx], preferred_element_type=jnp.float32), "tp")
                hidden = hidden + mix_out + b_out[layer_idx]
                inner_act = jax.nn.gelu(jnp.dot(layer_norm(hidden).astype(jnp.bfloat16), w_up[layer_idx], preferred_element_type=jnp.float32)).astype(jnp.bfloat16)
                hidden = hidden + lax.psum(jnp.dot(inner_act, w_down[layer_idx], preferred_element_type=jnp.float32), "tp")
            hidden_rows.append(hidden)
        return (jnp.stack(hidden_rows), v_all, z_all, jnp.stack(states))

    specs_in = (
        P(None, "dp", None),
        P(None, "dp", "sp", "tp"),
        P(None, "dp", "sp", "tp"),
        P(None, "dp", None, None, "tp"),
        P(None, None, None, "tp"),
        P(None, None, "tp"),
        P(None, None, None, "tp"),
        P(None, None, None, "tp"),
        P(None, None, "tp"),
        P(None, "tp", None),
        P(None, None),
        P(None, None, "tp"),
        P(None, "tp", None),
    )
    specs_out = (
        P(None, "dp", None),
        P(None, "dp", "sp", "tp"),
        P(None, "dp", "sp", "tp"),
        P(None, "dp", None, None, "tp"),
    )
    return jax.shard_map(device_fn, mesh=mesh, in_specs=specs_in, out_specs=specs_out, check_vma=False)
```

profile of v0, /device:TPU:0, one launch (start us, length us, event | category | flops | bytes accessed | tf_op | source)
XLA Modules:
  0.0 868.4 jit_solution(5214748384088809823)
XLA Ops:
  11.8 20.7 %copy.54 = bf16[2,2,4096,192]{3,1,2,0:T(2,128)(2,1)} copy(bf16[2,2,4096,192]{2,3,1,0:T(8,128)(2,1)} %param.14) | data formatting | bytes 12582912 | tf_op args[1]
  33.8 92.2 %copy.55 = f32[2,2,16384,192]{3,1,2,0:T(2,128)} copy(f32[2,2,16384,192]{2,3,1,0:T(8,128)} %param.20) | data formatting | bytes 100663296 | tf_op args[7]
  126.0 38.0 %gather_fusion = f32[4099,2,2,192]{3,2,1,0:T(2,128)} fusion(f32[2,2,16384,192]{3,1,2,0:T(2,128)} %copy.55, s32[5120]{0:T(1024)S(1)} %pad_clamp_fusion), kind=kCustom, calls=%fused_computation | custom fusion | bytes 25200652 | tf_op jit(solution)/shard_map/jit(_take)/gather | solution.py:19
  164.0 26.9 %select_bitcast_fusion = f32[2,2,4099,192]{3,1,0,2:T(2,128)} fusion(f32[4099,2,2,192]{3,2,1,0:T(2,128)} %gather_fusion, pred[4099]{0:T(1024)(128)(4,1)S(1)} %get-tuple-element.144, pred[4099]{0:T(1024)(128)(4,1)S(1)} %get-tuple-element.143), kind=kLoop, calls=%fused_computation.1 | loop fusion | flops 6296064 | bytes 25192454 | tf_op jit(solution)/shard_map/jit(_where)/select_n | solution.py:20
  191.0 74.7 %fusion.447 = (f32[1,1,4096,192]{3,1,0,2:T(1,128)}, f32[1,1,4096,192]{3,1,0,2:T(1,128)}, f32[1,1,4096,192]{3,1,0,2:T(1,128)}, f32[1,1,4096,192]{3,1,0,2:T(1,128)...) fusion(f32[2,2,4099,192]{3,1,0,2:T(2,128)} %select_bitcast_fusion), kind=kLoop, calls=%fused_computation.623 | loop fusion | bytes 100663296 | tf_op jit(solution)/shard_map/slice | solution.py:66
  268.1 10.0 %fusion.15 = f32[2,192]{1,0:T(2,128)S(1)} fusion(bf16[2,2,4096,192]{3,1,2,0:T(2,128)(2,1)} %constant_dynamic-update-slice_fusion.15, f32[4096,192]{1,0:T(8,128)S(1)} %bitcast.611), kind=kLoop, calls=%fused_computation.33 | loop fusion | flops 4718208 | bytes 6292992 | tf_op jit(solution)/shard_map/reduce_sum | solution.py:62
  278.1 123.8 %psum.224 = f32[2,192]{1,0:T(2,128)S(1)} all-reduce(f32[2,192]{1,0:T(2,128)S(1)} %fusion.15), channel_id=1, replica_groups=mesh['dp'=2,'tp'=4,'sp'=4] {'sp'}, use_global_device_ids=true, to_apply=%region_3.4 | all-reduce | flops 384 | bytes 3072 | tf_op jit(solution)/shard_map/psum | solution.py:63
  401.9 20.7 %copy.59 = bf16[2,2,4096,192]{3,1,2,0:T(2,128)(2,1)} copy(bf16[2,2,4096,192]{2,3,1,0:T(8,128)(2,1)} %param.15) | data formatting | bytes 12582912 | tf_op args[2]
  428.4 8.8 %fusion.14 = f32[2,192]{1,0:T(2,128)S(1)} fusion(bf16[2,2,4096,192]{3,1,2,0:T(2,128)(2,1)S(1)} %copy-done, f32[4096,192]{1,0:T(8,128)S(1)} %bitcast.612), kind=kLoop, calls=%fused_computation.31 | loop fusion | flops 4718208 | bytes 6292992 | tf_op jit(solution)/shard_map/reduce_sum | solution.py:66
  443.1 12.2 %psum.226 = f32[2,768]{1,0:T(2,128)S(1)} all-reduce(f32[2,768]{1,0:T(2,128)S(1)} %fusion.106), channel_id=1, replica_groups=mesh['dp'=2,'tp'=4,'sp'=4] {'tp'}, use_global_device_ids=true, to_apply=%region_6.7 | all-reduce | flops 1536 | bytes 12288 | tf_op jit(solution)/shard_map/psum | solution.py:69
  473.8 8.7 %fusion.13 = f32[2,192]{1,0:T(2,128)S(1)} fusion(bf16[2,2,4096,192]{3,1,2,0:T(2,128)(2,1)S(1)} %copy-done.8, f32[4096,192]{1,0:T(8,128)S(1)} %bitcast.613), kind=kLoop, calls=%fused_computation.29 | loop fusion | flops 4718208 | bytes 6292992 | tf_op jit(solution)/shard_map/reduce_sum | solution.py:62
  488.4 8.7 %fusion.11 = f32[2,192]{1,0:T(2,128)S(1)} fusion(bf16[2,2,4096,192]{3,1,2,0:T(2,128)(2,1)S(1)} %copy-done.9, f32[4096,192]{1,0:T(8,128)S(1)} %bitcast.614), kind=kLoop, calls=%fused_computation.25 | loop fusion | flops 4718208 | bytes 6292992 | tf_op jit(solution)/shard_map/reduce_sum | solution.py:62
  508.8 8.7 %fusion.12 = f32[2,192]{1,0:T(2,128)S(1)} fusion(bf16[2,2,4096,192]{3,1,2,0:T(2,128)(2,1)S(1)} %copy-done.1, f32[4096,192]{1,0:T(8,128)S(1)} %bitcast.615), kind=kLoop, calls=%fused_computation.27 | loop fusion | flops 4718208 | bytes 6292992 | tf_op jit(solution)/shard_map/reduce_sum | solution.py:66
  520.8 8.7 %fusion.10 = f32[2,192]{1,0:T(2,128)S(1)} fusion(bf16[2,2,4096,192]{3,1,2,0:T(2,128)(2,1)S(1)} %get-tuple-element.74, f32[4096,192]{1,0:T(8,128)S(1)} %bitcast.616), kind=kLoop, calls=%fused_computation.23 | loop fusion | flops 4718208 | bytes 6292992 | tf_op jit(solution)/shard_map/reduce_sum | solution.py:66
  535.4 10.5 %psum.234 = f32[2,768]{1,0:T(2,128)S(1)} all-reduce(f32[2,768]{1,0:T(2,128)S(1)} %fusion.104), channel_id=1, replica_groups=mesh['dp'=2,'tp'=4,'sp'=4] {'tp'}, use_global_device_ids=true, to_apply=%region_26.27 | all-reduce | flops 1536 | bytes 12288 | tf_op jit(solution)/shard_map/psum | solution.py:69
  564.4 8.9 %fusion.9 = f32[2,192]{1,0:T(2,128)S(1)} fusion(bf16[2,2,4096,192]{3,1,2,0:T(2,128)(2,1)S(1)} %copy-done.10, f32[4096,192]{1,0:T(8,128)S(1)} %bitcast.617), kind=kLoop, calls=%fused_computation.21 | loop fusion | flops 4718208 | bytes 6292992 | tf_op jit(solution)/shard_map/reduce_sum | solution.py:62
  579.2 8.7 %fusion.7 = f32[2,192]{1,0:T(2,128)S(1)} fusion(bf16[2,2,4096,192]{3,1,2,0:T(2,128)(2,1)S(1)} %copy-done.11, f32[4096,192]{1,0:T(8,128)S(1)} %bitcast.618), kind=kLoop, calls=%fused_computation.17 | loop fusion | flops 4718208 | bytes 6292992 | tf_op jit(solution)/shard_map/reduce_sum | solution.py:62
  627.1 10.5 %psum.242 = f32[2,768]{1,0:T(2,128)S(1)} all-reduce(f32[2,768]{1,0:T(2,128)S(1)} %fusion.102), channel_id=1, replica_groups=mesh['dp'=2,'tp'=4,'sp'=4] {'tp'}, use_global_device_ids=true, to_apply=%region_46.47 | all-reduce | flops 1536 | bytes 12288 | tf_op jit(solution)/shard_map/psum | solution.py:69
  703.2 8.7 %fusion.2 = f32[2,192]{1,0:T(2,128)S(1)} fusion(bf16[2,2,4096,192]{3,1,2,0:T(2,128)(2,1)S(1)} %get-tuple-element.58, f32[4096,192]{1,0:T(8,128)S(1)} %bitcast.624), kind=kLoop, calls=%fused_computation.7 | loop fusion | flops 4718208 | bytes 6292992 | tf_op jit(solution)/shard_map/reduce_sum | solution.py:66
  718.2 10.5 %psum.250 = f32[2,768]{1,0:T(2,128)S(1)} all-reduce(f32[2,768]{1,0:T(2,128)S(1)} %fusion.100), channel_id=1, replica_groups=mesh['dp'=2,'tp'=4,'sp'=4] {'tp'}, use_global_device_ids=true, to_apply=%region_66.67 | all-reduce | flops 1536 | bytes 12288 | tf_op jit(solution)/shard_map/psum | solution.py:69
  763.5 20.6 %copy.92 = bf16[2,2,4096,192]{2,3,1,0:T(8,128)(2,1)} copy(bf16[2,2,4096,192]{3,1,2,0:T(2,128)(2,1)} %get-tuple-element.52) | data formatting | bytes 12582912
  804.9 17.6 %all-reduce.5 = (f32[2,768]{1,0:T(2,128)S(1)}, f32[2,768]{1,0:T(2,128)S(1)}, f32[2,768]{1,0:T(2,128)S(1)}, f32[2,768]{1,0:T(2,128)S(1)}) all-reduce(f32[2,768]{1,0:T(2,128)S(1)} %fusion.92, f32[2,768]{1,0:T(2,128)S(1)} %fusion.94, f32[2,768]{1,0:T(2,128)S(1)} %fusion.96, ...), channel_id=1, replica_groups=mesh['dp'=2,'tp'=4,'sp'=4] {'tp'}, use_global_device_ids=true, to_apply=%region_76.77 | all-reduce | flops 6144 | bytes 49152 | tf_op jit(solution)/shard_map/psum | solution.py:69
  831.0 15.8 %all-reduce.4 = (f32[2,768]{1,0:T(2,128)S(1)}, f32[2,768]{1,0:T(2,128)S(1)}, f32[2,768]{1,0:T(2,128)S(1)}, f32[2,768]{1,0:T(2,128)S(1)}) all-reduce(f32[2,768]{1,0:T(2,128)S(1)} %fusion.16, f32[2,768]{1,0:T(2,128)S(1)} %fusion.18, f32[2,768]{1,0:T(2,128)S(1)} %fusion.20, ...), channel_id=1, replica_groups=mesh['dp'=2,'tp'=4,'sp'=4] {'tp'}, use_global_device_ids=true, to_apply=%region_79.80 | all-reduce | flops 6144 | bytes 49152 | tf_op jit(solution)/shard_map/psum | solution.py:72
  847.4 20.6 %copy.91 = bf16[2,2,4096,192]{2,3,1,0:T(8,128)(2,1)} copy(bf16[2,2,4096,192]{3,1,2,0:T(2,128)(2,1)} %constant_dynamic-update-slice_fusion.1) | data formatting | bytes 12582912
  (207 shorter events, 271.5 us)
Async XLA Ops:
  4.8 7.0 copy-start.23
  268.1 133.8 %copy-start.22 = (f32[2,2,192]{2,1,0:T(2,128)S(1)}, f32[2,2,192]{2,1,0:T(2,128)}, u32[]{:S(2)}) copy-start(f32[2,2,192]{2,1,0:T(2,128)} %param.21) | copy-start | bytes 9220
  423.8 4.6 copy-start
  428.4 14.5 %copy-start.18 = (bf16[2,192,768]{2,1,0:T(8,128)(2,1)S(1)}, bf16[2,192,768]{2,1,0:T(8,128)(2,1)}, u32[]{:S(2)}) copy-start(bf16[2,192,768]{2,1,0:T(8,128)(2,1)} %param.22) | copy-start | bytes 1769476
  428.4 26.9 %copy-start.21 = (f32[2,768]{1,0:T(2,128)S(1)}, f32[2,768]{1,0:T(2,128)}, u32[]{:S(2)}) copy-start(f32[2,768]{1,0:T(2,128)} %param.23) | copy-start | bytes 18436
  428.4 26.9 %copy-start.19 = (bf16[4,2,768]{2,1,0:T(2,128)(2,1)S(1)}, bf16[4,2,768]{2,1,0:T(2,128)(2,1)}, u32[]{:S(2)}) copy-start(bf16[4,2,768]{2,1,0:T(2,128)(2,1)} %param.13) | copy-start | bytes 36868
  428.4 27.2 %copy-start.26 = (bf16[2,768,768]{2,1,0:T(8,128)(2,1)S(1)}, bf16[2,768,768]{2,1,0:T(8,128)(2,1)}, u32[]{:S(2)}) copy-start(bf16[2,768,768]{2,1,0:T(8,128)(2,1)} %param.25) | copy-start | bytes 7077892
  469.2 4.6 copy-start.8
  483.8 4.6 copy-start.9
  504.2 4.6 copy-start.1
  508.8 8.8 %copy-start.17 = (f32[1,1,4096,192]{3,1,0,2:T(1,128)S(1)}, f32[1,1,4096,192]{3,1,0,2:T(1,128)}, u32[]{:S(2)}) copy-start(f32[1,1,4096,192]{3,1,0,2:T(1,128)} %get-tuple-element.95) | copy-start | bytes 9437188
  559.7 4.6 copy-start.10
  574.6 4.6 copy-start.11
  594.9 4.6 copy-start.3
  599.5 8.8 %copy-start.16 = (f32[1,1,4096,192]{3,1,0,2:T(1,128)S(1)}, f32[1,1,4096,192]{3,1,0,2:T(1,128)}, u32[]{:S(2)}) copy-start(f32[1,1,4096,192]{3,1,0,2:T(1,128)} %get-tuple-element.91) | copy-start | bytes 9437188
  651.4 4.6 copy-start.12
  656.0 8.7 %copy-start.20 = (f32[2,3,192]{2,0,1:T(2,128)S(1)}, f32[2,3,192]{2,0,1:T(2,128)}, u32[]{:S(2)}) copy-start(f32[2,3,192]{2,0,1:T(2,128)} %get-tuple-element.103) | copy-start | bytes 13828
  666.0 4.6 copy-start.13
  686.6 4.6 copy-start.5
  691.2 8.8 %copy-start.15 = (f32[1,1,4096,192]{3,1,0,2:T(1,128)S(1)}, f32[1,1,4096,192]{3,1,0,2:T(1,128)}, u32[]{:S(2)}) copy-start(f32[1,1,4096,192]{3,1,0,2:T(1,128)} %get-tuple-element.87) | copy-start | bytes 9437188
  703.2 38.1 %copy-start.24 = (bf16[2,3,192]{2,0,1:T(2,128)(2,1)S(1)}, bf16[2,3,192]{2,0,1:T(2,128)(2,1)}, u32[]{:S(2)}) copy-start(bf16[2,3,192]{2,0,1:T(2,128)(2,1)} %copy-done.23) | copy-start | bytes 6916
  703.2 38.1 %copy-start.25 = (bf16[2,3,192]{2,0,1:T(2,128)(2,1)S(1)}, bf16[2,3,192]{2,0,1:T(2,128)(2,1)}, u32[]{:S(2)}) copy-start(bf16[2,3,192]{2,0,1:T(2,128)(2,1)} %get-tuple-element.124) | copy-start | bytes 6916
  743.2 4.6 copy-start.14
  784.1 4.6 copy-start.7
  (3 other events, 9.7 us)
where the time goes:
time: 884 us; the launch traced here: 868 us
  local copies, waits for them, and re-layouts  358 us (40%)
  blocking collectives  289 us (33%)
  other arithmetic  191 us (22%)
  matrix products  29 us (3%)
    unnamed x66, local copies, waits for them, and re-layouts  208 us
    psum x5, blocking collectives, device_fn(): lax.psum(part_one, 'sp')  147 us
    slice x1, local copies, waits for them, and re-layouts, device_fn(): windows[layer_idx, 1, win_start:win_start + shard_len][None]  74.7 us
    reduce_sum x8, other arithmetic, device_fn(): jnp.sum(v_all[layer_idx] * windows[layer_idx, 0, win_start:win_start + sh...  71.3 us
    reduce_sum x8, other arithmetic, device_fn(): jnp.sum(z_all[layer_idx] * windows[layer_idx, 1, win_start:win_start + sh...  69.8 us
    psum x5, blocking collectives, device_fn(): lax.psum(jnp.dot(y_row, w_out[layer_idx], preferred_element_type=jnp.floa...  61.3 us
    psum x5, blocking collectives, device_fn(): lax.psum(jnp.dot(inner_act, w_down[layer_idx], preferred_element_type=jnp...  49.7 us
    gather x1, local copies, waits for them, and re-layouts, filter_windows(): picked = jnp.take(long_filt, jnp.maximum(lag_pos, 0), axis=2)  38 us

commit v1 on v0

v1 whole, which is shorter than its diff:
```python
import functools

import jax
import jax.numpy as jnp
from jax import lax
from jax.experimental import pallas as pl
from jax.experimental.pallas import tpu as pltpu
from jax.sharding import PartitionSpec as P

STEPS = 4
LAYERS = 2
SEQ = 2
ROWS = STEPS * SEQ
LANES = 128
CHUNKS = 4
MESH = pl.DeviceIdType.MESH


def layer_norm(rows_in):
    mean_val = jnp.mean(rows_in, axis=-1, keepdims=True)
    centered = rows_in - mean_val
    var_val = jnp.mean(centered * centered, axis=-1, keepdims=True)
    return centered * lax.rsqrt(var_val + 1e-5)


def kernel(e_hbm, v_hbm, z_hbm, st_hbm, win_hbm, bin_hbm, tap_hbm, h_hbm, skip_hbm, wout_hbm, bout_hbm, wup_hbm, wdown_hbm,
           hid_out, v_ref, z_ref, st_out,
           e_ref, st_ref, win, bin_ref, tap_ref, h_ref, lag_ref, skip_ref, wout, bout_ref, wup, wdown,
           acc, st8, newrow, hx, ar,
           small_sem, chunk_sem, w_sem, hsend, hrecv, asend, arecv, hid_sem):
    tp = lax.axis_index("tp")
    sp = lax.axis_index("sp")
    chan, shard_len = v_hbm.shape[2], v_hbm.shape[3]
    tiles = shard_len // LANES
    rows_per = chan // CHUNKS
    peers = [({"tp": lax.rem(tp + d, 4)}) for d in (1, 2, 3)]
    sp_peers = [({"sp": lax.rem(sp + d, 4)}) for d in (1, 2, 3)]

    barrier = pltpu.get_barrier_semaphore()
    for peer in peers + sp_peers:
        pl.semaphore_signal(barrier, inc=1, device_id=peer, device_id_type=MESH)

    smalls = [pltpu.make_async_copy(src, dst, small_sem.at[n]) for n, (src, dst) in enumerate((
        (e_hbm, e_ref), (st_hbm, st_ref), (bin_hbm, bin_ref), (tap_hbm, tap_ref), (skip_hbm, skip_ref), (bout_hbm, bout_ref),
        (h_hbm.at[:, :, :, pl.ds(0, LANES)], lag_ref)))]
    first = pl.multiple_of(lax.rem(5 - sp, 3) * shard_len, LANES)

    def chunk_copies(layer, k):
        rows = pl.ds(k * rows_per, rows_per)
        return [
            pltpu.make_async_copy(v_hbm.at[layer, :, rows, :], v_ref.at[layer, :, rows, :], chunk_sem.at[layer, k, 0]),
            pltpu.make_async_copy(z_hbm.at[layer, :, rows, :], z_ref.at[layer, :, rows, :], chunk_sem.at[layer, k, 1]),
            pltpu.make_async_copy(h_hbm.at[layer, :, rows, pl.ds(first, shard_len + LANES)], h_ref.at[layer, :, rows, :],
                                  chunk_sem.at[layer, k, 2]),
        ]

    def weight_copy(layer, n):
        src, dst = ((win_hbm, win), (wout_hbm, wout), (wup_hbm, wup), (wdown_hbm, wdown))[n]
        return pltpu.make_async_copy(src.at[layer], dst.at[layer], w_sem.at[layer, n])

    for copy in smalls:
        copy.start()
    for layer in range(LAYERS):
        for k in range(CHUNKS):
            for copy in chunk_copies(layer, k):
                copy.start()
        for n in range(4):
            weight_copy(layer, n).start()

    lane8 = lax.broadcasted_iota(jnp.int32, (8, LANES), 1)
    lane16 = lax.broadcasted_iota(jnp.int32, (16, LANES), 1)
    flip = [lax.rem(a - lane8 + 2 * LANES, LANES) for a in range(2)]

    def conv_group(cache, layer, which, row):
        accs = [[[None] * SEQ for _ in range(STEPS)] for _ in range(2)]

        def flipped(u, t):
            x = h_ref[layer, which, pl.ds(row + 8 * u, 8), LANES * t:LANES * (t + 1)]
            return [jnp.take_along_axis(x, flip[a], axis=1) for a in range(2)]

        def values(b, m):
            return cache[layer, b, pl.ds(row, 16), LANES * m:LANES * (m + 1)]

        zero = jnp.zeros((16, LANES), jnp.bfloat16)
        cur = [flipped(u, tiles) for u in range(2)]
        val = [values(b, 0) for b in range(SEQ)]
        rot = [pltpu.roll(val[b], LANES - 2, 1) for b in range(SEQ)]
        for b in range(SEQ):
            edge = jnp.where(lane16 >= LANES - 2, rot[b], zero).astype(jnp.float32)
            for u in range(2):
                for a in range(2):
                    accs[u][a + 2][b] = cur[u][a] * edge[8 * u:8 * u + 8]
        for m in range(tiles):
            nxt = [flipped(u, tiles - 1 - m) for u in range(2)]
            last = m == tiles - 1
            val_n = [None if last else values(b, m + 1) for b in range(SEQ)]
            rot_n = [zero if last else pltpu.roll(val_n[b], LANES - 2, 1) for b in range(SEQ)]
            here = [val[b].astype(jnp.float32) for b in range(SEQ)]
            ahead = [jnp.where(lane16 < LANES - 2, rot[b], rot_n[b]).astype(jnp.float32) for b in range(SEQ)]
            for u in range(2):
                for a in range(2):
                    taps = jnp.where(lane8 <= a, cur[u][a], nxt[u][a])
                    for b in range(SEQ):
                        p0 = taps * here[b][8 * u:8 * u + 8]
                        p2 = taps * ahead[b][8 * u:8 * u + 8]
                        accs[u][a][b] = p0 if m == 0 else accs[u][a][b] + p0
                        accs[u][a + 2][b] = accs[u][a + 2][b] + p2
            cur, val, rot = nxt, val_n, rot_n
        for u in range(2):
            for j in range(STEPS):
                for b in range(SEQ):
                    n = SEQ * j + b
                    acc[which, pl.ds(row + 8 * u, 8), LANES * n:LANES * (n + 1)] = accs[u][j][b]

    def conv(layer, k0, k1):
        def chunk(k, _):
            for copy in chunk_copies(layer, k):
                copy.wait()

            def group(g, _):
                row = pl.multiple_of(k * rows_per + g * 16, 16)
                conv_group(v_ref, layer, 0, row)
                conv_group(z_ref, layer, 1, row)
                return 0

            lax.fori_loop(0, rows_per // 16, group, 0)
            return 0

        lax.fori_loop(k0, k1, chunk, 0)

    lane_c = lax.broadcasted_iota(jnp.int32, (chan, LANES), 1)

    def hist_copies(layer):
        return [pltpu.make_async_remote_copy(hx.at[layer, sp], hx.at[layer, sp], hsend.at[layer, d], hrecv.at[layer, d],
                                             device_id=sp_peers[d], device_id_type=MESH) for d in (1, 0, 2)]

    def send_hist(layer):
        total = jnp.zeros((chan, LANES), jnp.float32)
        for which in range(2):
            for n in range(ROWS):
                part = jnp.sum(acc[which, :, LANES * n:LANES * (n + 1)], axis=1, keepdims=True)
                total = jnp.where(lane_c == which * ROWS + n, part, total)
        hx[layer, sp] = jnp.transpose(total)[:2 * ROWS]
        for copy in hist_copies(layer):
            copy.start()

    def sum_hist(layer):
        for copy in hist_copies(layer):
            copy.wait_recv()
        return ((hx[layer, 0] + hx[layer, 1]) + hx[layer, 2]) + hx[layer, 3]

    def sum_copies(n):
        return [pltpu.make_async_remote_copy(ar.at[n, tp], ar.at[n, tp], asend.at[n, d], arecv.at[n, d],
                                             device_id=peers[d], device_id_type=MESH) for d in (1, 0, 2)]

    def send_sum(n, part):
        ar[n, tp] = part
        for copy in sum_copies(n):
            copy.start()

    def take_sum(n):
        for copy in sum_copies(n):
            copy.wait_recv()
        return ((ar[n, 0] + ar[n, 1]) + ar[n, 2]) + ar[n, 3]

    row_c = lax.broadcasted_iota(jnp.int32, (ROWS, chan), 0)

    def project(layer, hidden):
        normed = layer_norm(hidden).astype(jnp.bfloat16)
        mixed = []
        for g in range(3):
            p = lax.dot_general(normed, win[layer, g], (((1,), (1,)), ((), ())), preferred_element_type=jnp.float32)
            p = (p + bin_ref[g, layer][None]).astype(jnp.bfloat16).astype(jnp.float32)
            for b in range(SEQ):
                pair = st_ref[layer, b, g].astype(jnp.float32)
                st8[b:b + 1, :] = pair[0:1]
                st8[SEQ + b:SEQ + b + 1, :] = pair[1:2]
            held = st8[...]
            prev1 = jnp.where(row_c < SEQ, pltpu.roll(held, ROWS - SEQ, 0), pltpu.roll(p, SEQ, 0))
            prev2 = jnp.where(row_c < 2 * SEQ, held, pltpu.roll(p, 2 * SEQ, 0))
            mixed.append(tap_ref[0, g, layer][None] * p + tap_ref[1, g, layer][None] * prev1 + tap_ref[2, g, layer][None] * prev2)
            for b in range(SEQ):
                for slot in range(2):
                    r = SEQ * (STEPS - 2 + slot) + b
                    st_out[layer, b, g, slot:slot + 1, :] = p[r:r + 1].astype(jnp.bfloat16)
        return mixed

    def recent(layer, which, rows_f):
        total = (lag[layer][which][0:1] + skip_ref[layer, which][None]) * rows_f
        for back in range(1, STEPS):
            shifted = jnp.where(row_c < SEQ * back, 0.0, pltpu.roll(rows_f, SEQ * back, 0))
            total = total + lag[layer][which][back:back + 1] * shifted
        return total

    def mixer(layer, mixed, hist):
        value = mixed[2].astype(jnp.bfloat16).astype(jnp.float32)
        long_one = hist[:ROWS] + recent(layer, 0, value)
        z_rows = (mixed[0] * long_one).astype(jnp.bfloat16).astype(jnp.float32)
        long_two = hist[ROWS:] + recent(layer, 1, z_rows)
        y_rows = (mixed[1] * long_two).astype(jnp.bfloat16)
        return value, z_rows, jnp.dot(y_rows, wout[layer], preferred_element_type=jnp.float32)

    def mlp(layer, hidden):
        up = jnp.dot(layer_norm(hidden).astype(jnp.bfloat16), wup[layer], preferred_element_type=jnp.float32)
        return jnp.dot(jax.nn.gelu(up).astype(jnp.bfloat16), wdown[layer], preferred_element_type=jnp.float32)

    def put_rows(layer, value, z_rows):
        for n, rows_f in enumerate((value, z_rows)):
            for b in range(SEQ):
                for j in range(STEPS):
                    r = SEQ * j + b
                    at = STEPS * (SEQ * n + b) + j
                    newrow[at:at + 1, 0:chan] = rows_f[r:r + 1]
        turned = jnp.transpose(newrow[...])[:chan]

        @pl.when(sp == 3)
        def _():
            for n, cache in enumerate((v_ref, z_ref)):
                for b in range(SEQ):
                    at = STEPS * (SEQ * n + b)
                    moved = turned if at == 0 else pltpu.roll(turned, LANES - at, 1)
                    cache[layer, b, :, 0:LANES] = jnp.where(lane_c < STEPS, moved, 0.0).astype(jnp.bfloat16)

    newrow[...] = jnp.zeros_like(newrow)
    st8[...] = jnp.zeros_like(st8)
    for copy in smalls:
        copy.wait()
    lag = [[jnp.transpose(lag_ref[layer, which])[:8] for which in range(2)] for layer in range(LAYERS)]
    hidden = jnp.concatenate([e_ref[j].astype(jnp.float32) for j in range(STEPS)], axis=0)

    conv(0, 0, CHUNKS)
    pl.semaphore_wait(barrier, 6)
    send_hist(0)
    weight_copy(0, 0).wait()
    mixed = project(0, hidden)
    weight_copy(0, 1).wait()
    value, z_rows, part = mixer(0, mixed, sum_hist(0))
    send_sum(0, part)
    conv(1, 0, CHUNKS // 2)
    weight_copy(0, 2).wait()
    weight_copy(0, 3).wait()
    hidden = hidden + take_sum(0) + bout_ref[0:1]
    send_sum(1, mlp(0, hidden))
    conv(1, CHUNKS // 2, CHUNKS)
    send_hist(1)
    put_rows(0, value, z_rows)
    weight_copy(1, 0).wait()
    hidden = hidden + take_sum(1)
    mixed = project(1, hidden)
    weight_copy(1, 1).wait()
    value, z_rows, part = mixer(1, mixed, sum_hist(1))
    send_sum(2, part)
    put_rows(1, value, z_rows)
    weight_copy(1, 2).wait()
    weight_copy(1, 3).wait()
    hidden = hidden + take_sum(2) + bout_ref[1:2]
    send_sum(3, mlp(1, hidden))
    hidden = hidden + take_sum(3)
    for j in range(STEPS):
        hid_out[j] = hidden[SEQ * j:SEQ * j + SEQ]
    for layer in range(LAYERS):
        for copy in hist_copies(layer):
            copy.wait_send()
    for n in range(4):
        for copy in sum_copies(n):
            copy.wait_send()


def solution(mesh):
    def device_fn(step_emb, v_cache, z_cache, short_state, w_in, b_in, short_taps, long_filt, skip_gain, w_out, b_out, w_up, w_down):
        chan = v_cache.shape[3]
        shard_len = v_cache.shape[2]
        model = step_emb.shape[2]
        args = (
            step_emb,
            jnp.swapaxes(v_cache, 2, 3),
            jnp.swapaxes(z_cache, 2, 3),
            jnp.transpose(short_state, (0, 1, 3, 2, 4)),
            jnp.transpose(w_in, (0, 2, 3, 1)),
            jnp.transpose(b_in, (1, 0, 2)),
            jnp.transpose(short_taps, (1, 2, 0, 3)),
            jnp.swapaxes(long_filt, 2, 3),
            skip_gain,
            w_out,
            b_out,
            w_up,
            w_down,
        )
        f32, bf16 = jnp.float32, jnp.bfloat16
        dma = pltpu.SemaphoreType.DMA
        hid, v_out, z_out, st_out = pl.pallas_call(
            kernel,
            out_shape=(
                jax.ShapeDtypeStruct(step_emb.shape, f32),
                pltpu.VMEM(args[1].shape, bf16),
                pltpu.VMEM(args[2].shape, bf16),
                jax.ShapeDtypeStruct(args[3].shape, bf16),
            ),
            in_specs=[pl.BlockSpec(memory_space=pl.ANY)] * 13,
            out_specs=[pl.BlockSpec(memory_space=pltpu.VMEM)] * 4,
            scratch_shapes=[
                pltpu.VMEM(step_emb.shape, bf16),
                pltpu.VMEM(args[3].shape, bf16),
                pltpu.VMEM(args[4].shape, bf16),
                pltpu.VMEM(args[5].shape, f32),
                pltpu.VMEM(args[6].shape, f32),
                pltpu.VMEM((LAYERS, 2, chan, shard_len + LANES), f32),
                pltpu.VMEM((LAYERS, 2, chan, LANES), f32),
                pltpu.VMEM(skip_gain.shape, f32),
                pltpu.VMEM(w_out.shape, bf16),
                pltpu.VMEM(b_out.shape, f32),
                pltpu.VMEM(w_up.shape, bf16),
                pltpu.VMEM(w_down.shape, bf16),
                pltpu.VMEM((2, chan, ROWS * LANES), f32),
                pltpu.VMEM((ROWS, chan), f32),
                pltpu.VMEM((LANES, 2 * LANES), f32),
                pltpu.VMEM((LAYERS, 4, 2 * ROWS, chan), f32),
                pltpu.VMEM((4, 4, ROWS, model), f32),
                dma((7,)),
                dma((LAYERS, CHUNKS, 3)),
                dma((LAYERS, 4)),
                dma((LAYERS, 3)),
                dma((LAYERS, 3)),
                dma((4, 3)),
                dma((4, 3)),
                dma,
            ],
            compiler_params=pltpu.CompilerParams(collective_id=0, has_side_effects=True, vmem_limit_bytes=40 * 1024 * 1024),
            name="decode",
        )(*args)
        return (hid, jnp.swapaxes(v_out, 2, 3), jnp.swapaxes(z_out, 2, 3), jnp.transpose(st_out, (0, 1, 3, 2, 4)))

    specs_in = (
        P(None, "dp", None),
        P(None, "dp", "sp", "tp"),
        P(None, "dp", "sp", "tp"),
        P(None, "dp", None, None, "tp"),
        P(None, None, None, "tp"),
        P(None, None, "tp"),
        P(None, None, None, "tp"),
        P(None, None, None, "tp"),
        P(None, None, "tp"),
        P(None, "tp", None),
        P(None, None),
        P(None, None, "tp"),
        P(None, "tp", None),
    )
    specs_out = (
        P(None, "dp", None),
        P(None, "dp", "sp", "tp"),
        P(None, "dp", "sp", "tp"),
        P(None, "dp", None, None, "tp"),
    )
    return jax.shard_map(device_fn, mesh=mesh, in_specs=specs_in, out_specs=specs_out, check_vma=False)
```

time: 884 us -> 50.3 us (0.06); the launches traced: 868 us -> 49.9 us
  local copies, waits for them, and re-layouts: 358 us -> 11.9 us
  blocking collectives: 289 us -> 0 us
  other arithmetic: 191 us -> 0 us
  Pallas kernels: 0 us -> 37.3 us
  matrix products: 29 us -> 0 us
    psum x20 -> x0, blocking collectives: 289 us -> none  [the longest x5 147 us: device_fn(): lax.psum(part_one, 'sp')]
    unnamed x66 -> x18, local copies, waits for them, and re-layouts: 208 us -> 11.9 us
    reduce_sum x39 -> x0, other arithmetic: 146 us -> none  [the longest x8 71.3 us: device_fn(): jnp.sum(v_all[layer_idx] * windows[layer_idx, 0, win_start:win_start + sh...]
    slice x6 -> x0, local copies, waits for them, and re-layouts: 77 us -> none  [the longest x1 74.7 us: device_fn(): windows[layer_idx, 1, win_start:win_start + shard_len][None]]
    gather x1 -> x0, local copies, waits for them, and re-layouts: 38 us -> none  [filter_windows(): picked = jnp.take(long_filt, jnp.maximum(lag_pos, 0), axis=2)]
    pallas_call x0 -> x1, Pallas kernels: none -> 37.3 us  [device_fn(): pl.pallas_call(kernel, out_shape=(jax.ShapeDtypeStruct(step_emb.shape, f3...]
    mul x16 -> x0, local copies, waits for them, and re-layouts: 34.7 us -> none  [the longest x8 20.8 us: device_fn(): v_all[layer_idx]]
    dot_general x24 -> x0, matrix products: 29 us -> none  [the longest x8 14.8 us: device_fn(): jnp.dot(inner_act, w_down[layer_idx], preferred_element_type=jnp.float32)]
where the time goes in v1:
time: 50.3 us; the launch traced here: 49.9 us
  Pallas kernels  37.3 us (74%)
  local copies, waits for them, and re-layouts  11.9 us (24%)
  between operations  0.66 us (1%)
    pallas_call x1, Pallas kernels, device_fn(): pl.pallas_call(kernel, out_shape=(jax.ShapeDtypeStruct(step_emb.shape, f3...  37.3 us
    unnamed x18, local copies, waits for them, and re-layouts  11.9 us

profile of v1, /device:TPU:0, one launch (start us, length us, event | category | flops | bytes accessed | tf_op | source)
XLA Modules:
  0.0 49.9 jit_solution(14373515964257245522)
XLA Ops:
  0.6 0.0 copy-start
  0.6 1.1 %copy-done = bf16[2,192,768]{2,1,0:T(8,128)(2,1)S(1)} copy-done((bf16[2,192,768]{2,1,0:T(8,128)(2,1)S(1)}, bf16[2,192,768]{2,1,0:T(8,128)(2,1)}, u32[]{:S(2)}) %copy-start) | copy-done | bytes 589848
  1.7 0.0 copy-start.1
  1.7 0.7 %copy-done.1 = f32[2,3,3,192]{3,0,2,1:T(2,128)S(1)} copy-done((f32[2,3,3,192]{3,0,2,1:T(2,128)S(1)}, f32[2,3,3,192]{3,0,2,1:T(2,128)}, u32[]{:S(2)}) %copy-start.1) | copy-done | bytes 13848
  2.4 0.0 copy-start.2
  2.4 0.7 %copy-done.2 = bf16[4,2,768]{2,1,0:T(2,128)(2,1)S(1)} copy-done((bf16[4,2,768]{2,1,0:T(2,128)(2,1)S(1)}, bf16[4,2,768]{2,1,0:T(2,128)(2,1)}, u32[]{:S(2)}) %copy-start.2) | copy-done | bytes 12312
  3.1 0.0 copy-start.3
  3.1 0.7 %copy-done.3 = bf16[2,2,2,3,192]{4,2,3,1,0:T(2,128)(2,1)S(1)} copy-done((bf16[2,2,2,3,192]{4,2,3,1,0:T(2,128)(2,1)S(1)}, bf16[2,2,2,3,192]{4,2,3,1,0:T(2,128)(2,1)}, u32[]{:S(2)}) %copy-start.3) | copy-done | bytes 9240
  3.8 0.0 copy-start.4
  3.8 0.7 %copy-done.4 = f32[2,3,192]{2,0,1:T(2,128)S(1)} copy-done((f32[2,3,192]{2,0,1:T(2,128)S(1)}, f32[2,3,192]{2,0,1:T(2,128)}, u32[]{:S(2)}) %copy-start.4) | copy-done | bytes 4632
  4.5 0.0 copy-start.5
  4.5 0.7 %copy-done.5 = f32[2,768]{1,0:T(2,128)S(1)} copy-done((f32[2,768]{1,0:T(2,128)S(1)}, f32[2,768]{1,0:T(2,128)}, u32[]{:S(2)}) %copy-start.5) | copy-done | bytes 6168
  5.2 0.0 copy-start.6
  5.2 0.7 %copy-done.6 = f32[2,2,192]{2,1,0:T(2,128)S(1)} copy-done((f32[2,2,192]{2,1,0:T(2,128)S(1)}, f32[2,2,192]{2,1,0:T(2,128)}, u32[]{:S(2)}) %copy-start.6) | copy-done | bytes 3096
  5.9 37.3 %decode.1 = (f32[4,2,768]{2,1,0:T(2,128)S(1)}, bf16[2,2,192,4096]{3,2,1,0:T(8,128)(2,1)S(1)}, bf16[2,2,192,4096]{3,2,1,0:T(8,128)(2,1)S(1)}, bf16[2,2,3,2,192]{4,3,2,1,0:T(2,128)(2,1)S(1)}) custom-call(bf16[4,2,768]{2,1,0:T(2,128)(2,1)S(1)} %copy-done.2, bf16[2,2,192,4096]{3,2,1,0:T(8,128)(2,1)} %bitcast.17, bf16[2,2,192,4096]{3,2,1,0:T(8,128)(2,1)} %bitcast.18, ...), custom_call_target="tpu_custom_call" | custom-call | tf_op jit(solution)/shard_map/decode/pallas_call | solution.py:291
  43.3 2.7 %copy.21 = bf16[2,2,4096,192]{2,3,1,0:T(8,128)(2,1)} copy(bf16[2,2,4096,192]{2,3,1,0:T(8,128)(2,1)S(1)} %bitcast.11) | data formatting | bytes 12582912
  46.0 2.7 %copy.22 = bf16[2,2,4096,192]{2,3,1,0:T(8,128)(2,1)} copy(bf16[2,2,4096,192]{2,3,1,0:T(8,128)(2,1)S(1)} %bitcast.10) | data formatting | bytes 12582912
  48.7 0.6 %copy.23 = f32[4,2,768]{2,1,0:T(2,128)} copy(f32[4,2,768]{2,1,0:T(2,128)S(1)} %get-tuple-element.20) | data formatting | bytes 49152
  49.3 0.6 %copy.24 = bf16[2,2,2,3,192]{4,2,3,1,0:T(2,128)(2,1)} copy(bf16[2,2,2,3,192]{4,2,3,1,0:T(2,128)(2,1)S(1)} %bitcast.13) | data formatting | bytes 18432
Async XLA Ops:
  0.6 1.1 %copy-start = (bf16[2,192,768]{2,1,0:T(8,128)(2,1)S(1)}, bf16[2,192,768]{2,1,0:T(8,128)(2,1)}, u32[]{:S(2)}) copy-start(bf16[2,192,768]{2,1,0:T(8,128)(2,1)} %wout_hbm.1) | copy-start | bytes 1769476
  1.7 0.7 %copy-start.1 = (f32[2,3,3,192]{3,0,2,1:T(2,128)S(1)}, f32[2,3,3,192]{3,0,2,1:T(2,128)}, u32[]{:S(2)}) copy-start(f32[2,3,3,192]{3,0,2,1:T(2,128)} %param.19) | copy-start | bytes 41476
  2.4 0.7 %copy-start.2 = (bf16[4,2,768]{2,1,0:T(2,128)(2,1)S(1)}, bf16[4,2,768]{2,1,0:T(2,128)(2,1)}, u32[]{:S(2)}) copy-start(bf16[4,2,768]{2,1,0:T(2,128)(2,1)} %e_hbm.1) | copy-start | bytes 36868
  3.1 0.7 %copy-start.3 = (bf16[2,2,2,3,192]{4,2,3,1,0:T(2,128)(2,1)S(1)}, bf16[2,2,2,3,192]{4,2,3,1,0:T(2,128)(2,1)}, u32[]{:S(2)}) copy-start(bf16[2,2,2,3,192]{4,2,3,1,0:T(2,128)(2,1)} %param.16) | copy-start | bytes 27652
  3.8 0.7 %copy-start.4 = (f32[2,3,192]{2,0,1:T(2,128)S(1)}, f32[2,3,192]{2,0,1:T(2,128)}, u32[]{:S(2)}) copy-start(f32[2,3,192]{2,0,1:T(2,128)} %param.18) | copy-start | bytes 13828
  4.5 0.7 %copy-start.5 = (f32[2,768]{1,0:T(2,128)S(1)}, f32[2,768]{1,0:T(2,128)}, u32[]{:S(2)}) copy-start(f32[2,768]{1,0:T(2,128)} %bout_hbm.1) | copy-start | bytes 18436
  5.2 0.7 %copy-start.6 = (f32[2,2,192]{2,1,0:T(2,128)S(1)}, f32[2,2,192]{2,1,0:T(2,128)}, u32[]{:S(2)}) copy-start(f32[2,2,192]{2,1,0:T(2,128)} %skip_hbm.1) | copy-start | bytes 9220

commit v2 on v1

--- a/solution.py
+++ b/solution.py
@@ -12,7 +12,8 @@
 SEQ = 2
 ROWS = STEPS * SEQ
 LANES = 128
-CHUNKS = 4
+CHUNKS = 12
+SPLIT = 7
 MESH = pl.DeviceIdType.MESH
 
 
@@ -26,18 +27,24 @@
 def kernel(e_hbm, v_hbm, z_hbm, st_hbm, win_hbm, bin_hbm, tap_hbm, h_hbm, skip_hbm, wout_hbm, bout_hbm, wup_hbm, wdown_hbm,
            hid_out, v_ref, z_ref, st_out,
            e_ref, st_ref, win, bin_ref, tap_ref, h_ref, lag_ref, skip_ref, wout, bout_ref, wup, wdown,
-           acc, st8, newrow, hx, ar,
-           small_sem, chunk_sem, w_sem, hsend, hrecv, asend, arecv, hid_sem):
+           acc, prow, rrow, newrow, hx, ar, xb, fin,
+           small_sem, chunk_sem, w_sem, hsend, hrecv, asend, arecv, xsem, fsem):
     tp = lax.axis_index("tp")
     sp = lax.axis_index("sp")
+    core = lax.rem(sp, 2)
     chan, shard_len = v_hbm.shape[2], v_hbm.shape[3]
+    model = e_hbm.shape[2]
     tiles = shard_len // LANES
     rows_per = chan // CHUNKS
-    peers = [({"tp": lax.rem(tp + d, 4)}) for d in (1, 2, 3)]
-    sp_peers = [({"sp": lax.rem(sp + d, 4)}) for d in (1, 2, 3)]
+    half = lax.div(tp, 2)
+    near = tp + 1 - 2 * lax.rem(tp, 2)
+    peers = [{"tp": 3 - 3 * half}, {"tp": 2 - half}, {"tp": near}]
+    across = lax.rem(sp + 2, 4)
+    sp_peers = [(across, core), (across + 1 - 2 * core, 1 - core), (sp + 1 - 2 * core, 1 - core)]
+    partner = {"sp": sp + 1 - 2 * core}
 
     barrier = pltpu.get_barrier_semaphore()
-    for peer in peers + sp_peers:
+    for peer in peers + [{"sp": other} for other, _ in sp_peers]:
         pl.semaphore_signal(barrier, inc=1, device_id=peer, device_id_type=MESH)
 
     smalls = [pltpu.make_async_copy(src, dst, small_sem.at[n]) for n, (src, dst) in enumerate((
@@ -46,7 +53,7 @@
     first = pl.multiple_of(lax.rem(5 - sp, 3) * shard_len, LANES)
 
     def chunk_copies(layer, k):
-        rows = pl.ds(k * rows_per, rows_per)
+        rows = pl.ds(k * rows_per if isinstance(k, int) else pl.multiple_of(k * rows_per, rows_per), rows_per)
         return [
             pltpu.make_async_copy(v_hbm.at[layer, :, rows, :], v_ref.at[layer, :, rows, :], chunk_sem.at[layer, k, 0]),
             pltpu.make_async_copy(z_hbm.at[layer, :, rows, :], z_ref.at[layer, :, rows, :], chunk_sem.at[layer, k, 1]),
@@ -58,11 +65,12 @@
         src, dst = ((win_hbm, win), (wout_hbm, wout), (wup_hbm, wup), (wdown_hbm, wdown))[n]
         return pltpu.make_async_copy(src.at[layer], dst.at[layer], w_sem.at[layer, n])
 
-    for copy in smalls:
-        copy.start()
     for layer in range(LAYERS):
         for k in range(CHUNKS):
             for copy in chunk_copies(layer, k):
+                copy.start()
+        if layer == 0:
+            for copy in smalls:
                 copy.start()
         for n in range(4):
             weight_copy(layer, n).start()
@@ -131,27 +139,38 @@
     lane_c = lax.broadcasted_iota(jnp.int32, (chan, LANES), 1)
 
     def hist_copies(layer):
-        return [pltpu.make_async_remote_copy(hx.at[layer, sp], hx.at[layer, sp], hsend.at[layer, d], hrecv.at[layer, d],
-                                             device_id=sp_peers[d], device_id_type=MESH) for d in (1, 0, 2)]
+        return [pltpu.make_async_remote_copy(hx.at[layer, sp, seq], hx.at[layer, sp, seq], hsend.at[layer, d], hrecv.at[layer, sp],
+                                             device_id={"sp": other}, device_id_type=MESH)
+                for d, (other, seq) in enumerate(sp_peers)]
 
     def send_hist(layer):
         total = jnp.zeros((chan, LANES), jnp.float32)
         for which in range(2):
-            for n in range(ROWS):
-                part = jnp.sum(acc[which, :, LANES * n:LANES * (n + 1)], axis=1, keepdims=True)
-                total = jnp.where(lane_c == which * ROWS + n, part, total)
-        hx[layer, sp] = jnp.transpose(total)[:2 * ROWS]
-        for copy in hist_copies(layer):
-            copy.start()
+            for j in range(STEPS):
+                for b in range(SEQ):
+                    n = SEQ * j + b
+                    part = jnp.sum(acc[which, :, LANES * n:LANES * (n + 1)], axis=1, keepdims=True)
+                    total = jnp.where(lane_c == (2 * b + which) * STEPS + j, part, total)
+        turned = jnp.transpose(total)
+        for b in range(SEQ):
+            hx[layer, sp, b] = turned[2 * STEPS * b:2 * STEPS * (b + 1)]
+
+        @pl.when(sp != 3)
+        def _():
+            for copy in hist_copies(layer):
+                copy.start()
 
     def sum_hist(layer):
-        for copy in hist_copies(layer):
-            copy.wait_recv()
-        return ((hx[layer, 0] + hx[layer, 1]) + hx[layer, 2]) + hx[layer, 3]
+        for src in range(3):
+            @pl.when(sp != src)
+            def _():
+                pltpu.make_async_remote_copy(hx.at[layer, src, core], hx.at[layer, src, core], hsend.at[layer, 0], hrecv.at[layer, src],
+                                             device_id=partner, device_id_type=MESH).wait_recv()
+        return (hx[layer, 0, core] + hx[layer, 1, core]) + hx[layer, 2, core]
 
     def sum_copies(n):
-        return [pltpu.make_async_remote_copy(ar.at[n, tp], ar.at[n, tp], asend.at[n, d], arecv.at[n, d],
-                                             device_id=peers[d], device_id_type=MESH) for d in (1, 0, 2)]
+        return [pltpu.make_async_remote_copy(ar.at[n, tp], ar.at[n, tp], asend.at[n, d], arecv.at[n, tp],
+                                             device_id=peers[d], device_id_type=MESH) for d in range(3)]
 
     def send_sum(n, part):
         ar[n, tp] = part
@@ -159,11 +178,15 @@
             copy.start()
 
     def take_sum(n):
-        for copy in sum_copies(n):
-            copy.wait_recv()
+        for d in (1, 2, 3):
+            src = lax.rem(tp + d, 4)
+            pltpu.make_async_remote_copy(ar.at[n, src], ar.at[n, src], asend.at[n, 0], arecv.at[n, src],
+                                         device_id=peers[0], device_id_type=MESH).wait_recv()
         return ((ar[n, 0] + ar[n, 1]) + ar[n, 2]) + ar[n, 3]
 
-    row_c = lax.broadcasted_iota(jnp.int32, (ROWS, chan), 0)
+    def swap_copy(layer):
+        return pltpu.make_async_remote_copy(xb.at[layer, core], xb.at[layer, core], xsem.at[layer, 0], xsem.at[layer, 1],
+                                            device_id=partner, device_id_type=MESH)
 
     def project(layer, hidden):
         normed = layer_norm(hidden).astype(jnp.bfloat16)
@@ -171,99 +194,116 @@
         for g in range(3):
             p = lax.dot_general(normed, win[layer, g], (((1,), (1,)), ((), ())), preferred_element_type=jnp.float32)
             p = (p + bin_ref[g, layer][None]).astype(jnp.bfloat16).astype(jnp.float32)
-            for b in range(SEQ):
-                pair = st_ref[layer, b, g].astype(jnp.float32)
-                st8[b:b + 1, :] = pair[0:1]
-                st8[SEQ + b:SEQ + b + 1, :] = pair[1:2]
-            held = st8[...]
-            prev1 = jnp.where(row_c < SEQ, pltpu.roll(held, ROWS - SEQ, 0), pltpu.roll(p, SEQ, 0))
-            prev2 = jnp.where(row_c < 2 * SEQ, held, pltpu.roll(p, 2 * SEQ, 0))
-            mixed.append(tap_ref[0, g, layer][None] * p + tap_ref[1, g, layer][None] * prev1 + tap_ref[2, g, layer][None] * prev2)
-            for b in range(SEQ):
-                for slot in range(2):
-                    r = SEQ * (STEPS - 2 + slot) + b
-                    st_out[layer, b, g, slot:slot + 1, :] = p[r:r + 1].astype(jnp.bfloat16)
+            prow[layer, g, 0:2, :] = st_ref[layer, core, g].astype(jnp.float32)
+            prow[layer, g, 2:2 + STEPS, :] = p
+            mixed.append(tap_ref[0, g, layer][None] * p + tap_ref[1, g, layer][None] * prow[layer, g, 1:1 + STEPS, :]
+                         + tap_ref[2, g, layer][None] * prow[layer, g, 0:STEPS, :])
         return mixed
 
     def recent(layer, which, rows_f):
+        rrow[layer, which, STEPS - 1:2 * STEPS - 1, :] = rows_f
         total = (lag[layer][which][0:1] + skip_ref[layer, which][None]) * rows_f
         for back in range(1, STEPS):
-            shifted = jnp.where(row_c < SEQ * back, 0.0, pltpu.roll(rows_f, SEQ * back, 0))
-            total = total + lag[layer][which][back:back + 1] * shifted
+            total = total + lag[layer][which][back:back + 1] * rrow[layer, which, STEPS - 1 - back:2 * STEPS - 1 - back, :]
         return total
 
     def mixer(layer, mixed, hist):
         value = mixed[2].astype(jnp.bfloat16).astype(jnp.float32)
-        long_one = hist[:ROWS] + recent(layer, 0, value)
+        long_one = hist[:STEPS] + recent(layer, 0, value)
         z_rows = (mixed[0] * long_one).astype(jnp.bfloat16).astype(jnp.float32)
-        long_two = hist[ROWS:] + recent(layer, 1, z_rows)
+        long_two = hist[STEPS:] + recent(layer, 1, z_rows)
         y_rows = (mixed[1] * long_two).astype(jnp.bfloat16)
-        return value, z_rows, jnp.dot(y_rows, wout[layer], preferred_element_type=jnp.float32)
+        send_sum(2 * layer, jnp.dot(y_rows, wout[layer], preferred_element_type=jnp.float32))
+        for g in range(3):
+            xb[layer, core, 2 * g:2 * g + 2, :] = prow[layer, g, STEPS:STEPS + 2, :]
+        xb[layer, core, 6:8, :] = jnp.zeros((2, chan), jnp.float32)
+        xb[layer, core, 8:8 + STEPS, :] = value
+        xb[layer, core, 8 + STEPS:8 + 2 * STEPS, :] = z_rows
+        swap_copy(layer).start()
 
     def mlp(layer, hidden):
         up = jnp.dot(layer_norm(hidden).astype(jnp.bfloat16), wup[layer], preferred_element_type=jnp.float32)
         return jnp.dot(jax.nn.gelu(up).astype(jnp.bfloat16), wdown[layer], preferred_element_type=jnp.float32)
 
-    def put_rows(layer, value, z_rows):
-        for n, rows_f in enumerate((value, z_rows)):
-            for b in range(SEQ):
-                for j in range(STEPS):
-                    r = SEQ * j + b
-                    at = STEPS * (SEQ * n + b) + j
-                    newrow[at:at + 1, 0:chan] = rows_f[r:r + 1]
+    def put_rows(layer):
+        swap_copy(layer).wait_recv()
+        for b in range(SEQ):
+            newrow[2 * STEPS * b:2 * STEPS * (b + 1), 0:chan] = xb[layer, b, 8:16, :]
+            for g in range(3):
+                st_out[layer, b, g] = xb[layer, b, 2 * g:2 * g + 2, :].astype(jnp.bfloat16)
         turned = jnp.transpose(newrow[...])[:chan]
 
         @pl.when(sp == 3)
         def _():
-            for n, cache in enumerate((v_ref, z_ref)):
-                for b in range(SEQ):
-                    at = STEPS * (SEQ * n + b)
+            for b in range(SEQ):
+                for n, cache in enumerate((v_ref, z_ref)):
+                    at = STEPS * (2 * b + n)
                     moved = turned if at == 0 else pltpu.roll(turned, LANES - at, 1)
                     cache[layer, b, :, 0:LANES] = jnp.where(lane_c < STEPS, moved, 0.0).astype(jnp.bfloat16)
-
-    newrow[...] = jnp.zeros_like(newrow)
-    st8[...] = jnp.zeros_like(st8)
-    for copy in smalls:
-        copy.wait()
-    lag = [[jnp.transpose(lag_ref[layer, which])[:8] for which in range(2)] for layer in range(LAYERS)]
-    hidden = jnp.concatenate([e_ref[j].astype(jnp.float32) for j in range(STEPS)], axis=0)
 
     conv(0, 0, CHUNKS)
     pl.semaphore_wait(barrier, 6)
     send_hist(0)
+    newrow[...] = jnp.zeros_like(newrow)
+    rrow[...] = jnp.zeros_like(rrow)
+    for copy in smalls:
+        copy.wait()
+    hidden = jnp.where(core == 0, jnp.concatenate([e_ref[j].astype(jnp.float32)[0:1] for j in range(STEPS)], axis=0),
+                       jnp.concatenate([e_ref[j].astype(jnp.float32)[1:2] for j in range(STEPS)], axis=0))
+    lag = [[jnp.transpose(lag_ref[layer, which])[:8] for which in range(2)] for layer in range(LAYERS)]
     weight_copy(0, 0).wait()
     mixed = project(0, hidden)
     weight_copy(0, 1).wait()
-    value, z_rows, part = mixer(0, mixed, sum_hist(0))
-    send_sum(0, part)
-    conv(1, 0, CHUNKS // 2)
+    mixer(0, mixed, sum_hist(0))
+    conv(1, 0, SPLIT)
     weight_copy(0, 2).wait()
     weight_copy(0, 3).wait()
     hidden = hidden + take_sum(0) + bout_ref[0:1]
     send_sum(1, mlp(0, hidden))
-    conv(1, CHUNKS // 2, CHUNKS)
+    conv(1, SPLIT, CHUNKS)
     send_hist(1)
-    put_rows(0, value, z_rows)
     weight_copy(1, 0).wait()
     hidden = hidden + take_sum(1)
     mixed = project(1, hidden)
     weight_copy(1, 1).wait()
-    value, z_rows, part = mixer(1, mixed, sum_hist(1))
-    send_sum(2, part)
-    put_rows(1, value, z_rows)
+    mixer(1, mixed, sum_hist(1))
+    put_rows(0)
     weight_copy(1, 2).wait()
     weight_copy(1, 3).wait()
     hidden = hidden + take_sum(2) + bout_ref[1:2]
     send_sum(3, mlp(1, hidden))
+    put_rows(1)
     hidden = hidden + take_sum(3)
-    for j in range(STEPS):
-        hid_out[j] = hidden[SEQ * j:SEQ * j + SEQ]
+    fin[core] = hidden
+    last = pltpu.make_async_remote_copy(fin.at[core], fin.at[core], fsem.at[0], fsem.at[1], device_id=partner, device_id_type=MESH)
+    last.start()
     for layer in range(LAYERS):
-        for copy in hist_copies(layer):
-            copy.wait_send()
+        swap_copy(layer).wait_send()
+
+        @pl.when(sp != 3)
+        def _():
+            for copy in hist_copies(layer):
+                copy.wait_send()
     for n in range(4):
         for copy in sum_copies(n):
             copy.wait_send()
+    last.wait()
+    for b in range(SEQ):
+        for j in range(STEPS):
+            hid_out[j, b:b + 1, :] = fin[b, j:j + 1, :]
+
+
+def emit(hid, v, z, st, hid_o, v_o, z_o, st_o, sem):
+    copies = []
+    for layer in range(LAYERS):
+        for b in range(SEQ):
+            copies += [(v.at[layer, b], v_o.at[layer, b]), (z.at[layer, b], z_o.at[layer, b])]
+    copies += [(hid, hid_o), (st, st_o)]
+    copies = [pltpu.make_async_copy(src, dst, sem.at[n]) for n, (src, dst) in enumerate(copies)]
+    for copy in copies:
+        copy.start()
+    for copy in copies:
+        copy.wait()
 
 
 def solution(mesh):
@@ -286,6 +326,7 @@
             w_up,
             w_down,
         )
+        args = tuple(pltpu.with_memory_space_constraint(arg, pltpu.HBM) for arg in args)
         f32, bf16 = jnp.float32, jnp.bfloat16
         dma = pltpu.SemaphoreType.DMA
         hid, v_out, z_out, st_out = pl.pallas_call(
@@ -296,7 +337,7 @@
                 pltpu.VMEM(args[2].shape, bf16),
                 jax.ShapeDtypeStruct(args[3].shape, bf16),
             ),
-            in_specs=[pl.BlockSpec(memory_space=pl.ANY)] * 13,
+            in_specs=[pl.BlockSpec(memory_space=pltpu.HBM)] * 13,
             out_specs=[pl.BlockSpec(memory_space=pltpu.VMEM)] * 4,
             scratch_shapes=[
                 pltpu.VMEM(step_emb.shape, bf16),
@@ -312,22 +353,40 @@
                 pltpu.VMEM(w_up.shape, bf16),
                 pltpu.VMEM(w_down.shape, bf16),
                 pltpu.VMEM((2, chan, ROWS * LANES), f32),
-                pltpu.VMEM((ROWS, chan), f32),
+                pltpu.VMEM((LAYERS, 3, 8, chan), f32),
+                pltpu.VMEM((LAYERS, 2, 8, chan), f32),
                 pltpu.VMEM((LANES, 2 * LANES), f32),
-                pltpu.VMEM((LAYERS, 4, 2 * ROWS, chan), f32),
-                pltpu.VMEM((4, 4, ROWS, model), f32),
+                pltpu.VMEM((LAYERS, 4, SEQ, 2 * STEPS, chan), f32),
+                pltpu.VMEM((4, 4, STEPS, model), f32),
+                pltpu.VMEM((LAYERS, SEQ, 16, chan), f32),
+                pltpu.VMEM((SEQ, STEPS, model), f32),
                 dma((7,)),
                 dma((LAYERS, CHUNKS, 3)),
                 dma((LAYERS, 4)),
                 dma((LAYERS, 3)),
-                dma((LAYERS, 3)),
+                dma((LAYERS, 4)),
                 dma((4, 3)),
-                dma((4, 3)),
-                dma,
+                dma((4, 4)),
+                dma((LAYERS, 2)),
+                dma((2,)),
             ],
             compiler_params=pltpu.CompilerParams(collective_id=0, has_side_effects=True, vmem_limit_bytes=40 * 1024 * 1024),
             name="decode",
         )(*args)
+        hid, v_out, z_out, st_out = pl.pallas_call(
+            emit,
+            out_shape=(
+                jax.ShapeDtypeStruct(hid.shape, f32),
+                jax.ShapeDtypeStruct(v_out.shape, bf16),
+                jax.ShapeDtypeStruct(z_out.shape, bf16),
+                jax.ShapeDtypeStruct(st_out.shape, bf16),
+            ),
+            in_specs=[pl.BlockSpec(memory_space=pltpu.VMEM)] * 4,
+            out_specs=[pl.BlockSpec(memory_space=pltpu.HBM)] * 4,
+            scratch_shapes=[dma((4 * LAYERS + 2,))],
+            compiler_params=pltpu.CompilerParams(vmem_limit_bytes=1024 * 1024),
+            name="emit",
+        )(hid, v_out, z_out, st_out)
         return (hid, jnp.swapaxes(v_out, 2, 3), jnp.swapaxes(z_out, 2, 3), jnp.transpose(st_out, (0, 1, 3, 2, 4)))
 
     specs_in = (

time: 50.3 us -> 40.8 us (0.81)
  local copies, waits for them, and re-layouts: 11.9 us -> 0 us
  Pallas kernels: 37.3 us -> 40 us
    unnamed x18 -> x0, local copies, waits for them, and re-layouts: 11.9 us -> none
    pallas_call x0 -> x1, Pallas kernels: none -> 4.68 us  [device_fn(): pl.pallas_call(emit, out_shape=(jax.ShapeDtypeStruct(hid.shape, f32), jax...]
    pallas_call x1, Pallas kernels: 37.3 us -> 35.4 us  [device_fn(): pl.pallas_call(kernel, out_shape=(jax.ShapeDtypeStruct(step_emb.shape, f3...]
where the time goes in v2:
time: 40.8 us; the launch traced here: 40.7 us
  Pallas kernels  40 us (98%)
  between operations  0.64 us (2%)
    pallas_call x1, Pallas kernels, device_fn(): pl.pallas_call(kernel, out_shape=(jax.ShapeDtypeStruct(step_emb.shape, f3...  35.4 us
    pallas_call x1, Pallas kernels, device_fn(): pl.pallas_call(emit, out_shape=(jax.ShapeDtypeStruct(hid.shape, f32), jax...  4.68 us

profile of v2, /device:TPU:0, one launch (start us, length us, event | category | flops | bytes accessed | tf_op | source)
XLA Modules:
  0.0 40.7 jit_solution(10833371471002174365)
XLA Ops:
  0.6 35.4 %decode.1 = (f32[4,2,768]{2,1,0:T(2,128)S(1)}, bf16[2,2,192,4096]{3,2,1,0:T(8,128)(2,1)S(1)}, bf16[2,2,192,4096]{3,2,1,0:T(8,128)(2,1)S(1)}, bf16[2,2,3,2,192]{4,3,2,1,0:T(2,128)(2,1)S(1)}) custom-call(bf16[4,2,768]{2,1,0:T(2,128)(2,1)} %e_hbm.1, bf16[2,2,192,4096]{3,2,1,0:T(8,128)(2,1)} %bitcast.11, bf16[2,2,192,4096]{3,2,1,0:T(8,128)(2,1)} %bitcast.12, ...), custom_call_target="tpu_custom_call" | custom-call | tf_op jit(solution)/shard_map/decode/pallas_call | solution.py:332
  36.0 4.7 %emit.1 = (f32[4,2,768]{2,1,0:T(2,128)}, bf16[2,2,192,4096]{3,2,1,0:T(8,128)(2,1)}, bf16[2,2,192,4096]{3,2,1,0:T(8,128)(2,1)}, bf16[2,2,3,2,192]{4,3,2,1,0:T(2,128)(2,1)}) custom-call(f32[4,2,768]{2,1,0:T(2,128)S(1)} %get-tuple-element.12.hid, bf16[2,2,192,4096]{3,2,1,0:T(8,128)(2,1)S(1)} %get-tuple-element.13.v, ...), custom_call_target="tpu_custom_call" | custom-call | tf_op jit(solution)/shard_map/emit/pallas_call | solution.py:376

commit v3 on v2

--- a/solution.py
+++ b/solution.py
@@ -27,11 +27,13 @@
 def kernel(e_hbm, v_hbm, z_hbm, st_hbm, win_hbm, bin_hbm, tap_hbm, h_hbm, skip_hbm, wout_hbm, bout_hbm, wup_hbm, wdown_hbm,
            hid_out, v_ref, z_ref, st_out,
            e_ref, st_ref, win, bin_ref, tap_ref, h_ref, lag_ref, skip_ref, wout, bout_ref, wup, wdown,
-           acc, prow, rrow, newrow, hx, ar, xb, fin,
-           small_sem, chunk_sem, w_sem, hsend, hrecv, asend, arecv, xsem, fsem):
+           acc, total, lag, prow, rrow, newrow, hx, ar, xb, fin,
+           small_sem, chunk_sem, w_sem, hsend, hrecv, asend, arecv, xsend, xrecv, fsend, frecv):
     tp = lax.axis_index("tp")
     sp = lax.axis_index("sp")
-    core = lax.rem(sp, 2)
+    own = lax.div(sp, 2)
+    carries = lax.rem(sp, 2) == 1
+    has_rows = sp != 3
     chan, shard_len = v_hbm.shape[2], v_hbm.shape[3]
     model = e_hbm.shape[2]
     tiles = shard_len // LANES
@@ -39,13 +41,16 @@
     half = lax.div(tp, 2)
     near = tp + 1 - 2 * lax.rem(tp, 2)
     peers = [{"tp": 3 - 3 * half}, {"tp": 2 - half}, {"tp": near}]
-    across = lax.rem(sp + 2, 4)
-    sp_peers = [(across, core), (across + 1 - 2 * core, 1 - core), (sp + 1 - 2 * core, 1 - core)]
-    partner = {"sp": sp + 1 - 2 * core}
+    block_peers = [{"sp": lax.rem(sp + d, 4)} for d in (2, 3, 1)]
 
     barrier = pltpu.get_barrier_semaphore()
-    for peer in peers + [{"sp": other} for other, _ in sp_peers]:
+    for peer in block_peers:
         pl.semaphore_signal(barrier, inc=1, device_id=peer, device_id_type=MESH)
+
+    @pl.when(carries)
+    def _():
+        for peer in peers:
+            pl.semaphore_signal(barrier, inc=1, device_id=peer, device_id_type=MESH)
 
     smalls = [pltpu.make_async_copy(src, dst, small_sem.at[n]) for n, (src, dst) in enumerate((
         (e_hbm, e_ref), (st_hbm, st_ref), (bin_hbm, bin_ref), (tap_hbm, tap_ref), (skip_hbm, skip_ref), (bout_hbm, bout_ref),
@@ -120,53 +125,58 @@
                     n = SEQ * j + b
                     acc[which, pl.ds(row + 8 * u, 8), LANES * n:LANES * (n + 1)] = accs[u][j][b]
 
+    def close(row):
+        out = jnp.zeros((16, LANES), jnp.float32)
+        for which in range(2):
+            for j in range(STEPS):
+                for b in range(SEQ):
+                    n = SEQ * j + b
+                    part = jnp.sum(acc[which, pl.ds(row, 16), LANES * n:LANES * (n + 1)], axis=1, keepdims=True)
+                    out = jnp.where(lane16 == (2 * b + which) * STEPS + j, part, out)
+        total[pl.ds(row, 16), :] = out
+
     def conv(layer, k0, k1):
         def chunk(k, _):
             for copy in chunk_copies(layer, k):
                 copy.wait()
 
-            def group(g, _):
-                row = pl.multiple_of(k * rows_per + g * 16, 16)
+            @pl.when(has_rows)
+            def _():
+                row = pl.multiple_of(k * 16, 16)
                 conv_group(v_ref, layer, 0, row)
                 conv_group(z_ref, layer, 1, row)
-                return 0
-
-            lax.fori_loop(0, rows_per // 16, group, 0)
+
             return 0
 
         lax.fori_loop(k0, k1, chunk, 0)
 
     lane_c = lax.broadcasted_iota(jnp.int32, (chan, LANES), 1)
 
-    def hist_copies(layer):
-        return [pltpu.make_async_remote_copy(hx.at[layer, sp, seq], hx.at[layer, sp, seq], hsend.at[layer, d], hrecv.at[layer, sp],
-                                             device_id={"sp": other}, device_id_type=MESH)
-                for d, (other, seq) in enumerate(sp_peers)]
+    def hist_copy(layer, seq):
+        return pltpu.make_async_remote_copy(hx.at[layer, sp, seq], hx.at[layer, sp, seq], hsend.at[layer, seq], hrecv.at[layer, sp],
+                                            device_id={"sp": 2 * seq + 1}, device_id_type=MESH)
 
     def send_hist(layer):
-        total = jnp.zeros((chan, LANES), jnp.float32)
-        for which in range(2):
-            for j in range(STEPS):
-                for b in range(SEQ):
-                    n = SEQ * j + b
-                    part = jnp.sum(acc[which, :, LANES * n:LANES * (n + 1)], axis=1, keepdims=True)
-                    total = jnp.where(lane_c == (2 * b + which) * STEPS + j, part, total)
-        turned = jnp.transpose(total)
-        for b in range(SEQ):
-            hx[layer, sp, b] = turned[2 * STEPS * b:2 * STEPS * (b + 1)]
-
-        @pl.when(sp != 3)
+        @pl.when(has_rows)
         def _():
-            for copy in hist_copies(layer):
-                copy.start()
+            for row in range(0, chan, 16):
+                close(row)
+            turned = jnp.transpose(total[...])
+            for b in range(SEQ):
+                hx[layer, sp, b] = turned[2 * STEPS * b:2 * STEPS * (b + 1)]
+            hist_copy(layer, 1).start()
+
+            @pl.when(sp != 1)
+            def _():
+                hist_copy(layer, 0).start()
 
     def sum_hist(layer):
         for src in range(3):
             @pl.when(sp != src)
             def _():
-                pltpu.make_async_remote_copy(hx.at[layer, src, core], hx.at[layer, src, core], hsend.at[layer, 0], hrecv.at[layer, src],
-                                             device_id=partner, device_id_type=MESH).wait_recv()
-        return (hx[layer, 0, core] + hx[layer, 1, core]) + hx[layer, 2, core]
+                pltpu.make_async_remote_copy(hx.at[layer, src, own], hx.at[layer, src, own], hsend.at[layer, 0], hrecv.at[layer, src],
+                                             device_id=block_peers[0], device_id_type=MESH).wait_recv()
+        return (hx[layer, 0, own] + hx[layer, 1, own]) + hx[layer, 2, own]
 
     def sum_copies(n):
         return [pltpu.make_async_remote_copy(ar.at[n, tp], ar.at[n, tp], asend.at[n, d], arecv.at[n, tp],
@@ -184,9 +194,19 @@
                                          device_id=peers[0], device_id_type=MESH).wait_recv()
         return ((ar[n, 0] + ar[n, 1]) + ar[n, 2]) + ar[n, 3]
 
-    def swap_copy(layer):
-        return pltpu.make_async_remote_copy(xb.at[layer, core], xb.at[layer, core], xsem.at[layer, 0], xsem.at[layer, 1],
-                                            device_id=partner, device_id_type=MESH)
+    def row_copy(layer, seq, d):
+        return pltpu.make_async_remote_copy(xb.at[layer, seq], xb.at[layer, seq], xsend.at[layer, d], xrecv.at[layer, seq],
+                                            device_id=block_peers[d], device_id_type=MESH)
+
+    def row_copies(layer, seq):
+        return [row_copy(layer, seq, d) for d in range(3)]
+
+    def last_copy(seq, d):
+        return pltpu.make_async_remote_copy(fin.at[seq], fin.at[seq], fsend.at[d], frecv.at[seq],
+                                            device_id=block_peers[d], device_id_type=MESH)
+
+    def last_copies(seq):
+        return [last_copy(seq, d) for d in range(3)]
 
     def project(layer, hidden):
         normed = layer_norm(hidden).astype(jnp.bfloat16)
@@ -194,7 +214,7 @@
         for g in range(3):
             p = lax.dot_general(normed, win[layer, g], (((1,), (1,)), ((), ())), preferred_element_type=jnp.float32)
             p = (p + bin_ref[g, layer][None]).astype(jnp.bfloat16).astype(jnp.float32)
-            prow[layer, g, 0:2, :] = st_ref[layer, core, g].astype(jnp.float32)
+            prow[layer, g, 0:2, :] = st_ref[layer, own, g].astype(jnp.float32)
             prow[layer, g, 2:2 + STEPS, :] = p
             mixed.append(tap_ref[0, g, layer][None] * p + tap_ref[1, g, layer][None] * prow[layer, g, 1:1 + STEPS, :]
                          + tap_ref[2, g, layer][None] * prow[layer, g, 0:STEPS, :])
@@ -202,9 +222,9 @@
 
     def recent(layer, which, rows_f):
         rrow[layer, which, STEPS - 1:2 * STEPS - 1, :] = rows_f
-        total = (lag[layer][which][0:1] + skip_ref[layer, which][None]) * rows_f
+        total = (lag[layer, which, 0:1] + skip_ref[layer, which][None]) * rows_f
         for back in range(1, STEPS):
-            total = total + lag[layer][which][back:back + 1] * rrow[layer, which, STEPS - 1 - back:2 * STEPS - 1 - back, :]
+            total = total + lag[layer, which, back:back + 1] * rrow[layer, which, STEPS - 1 - back:2 * STEPS - 1 - back, :]
         return total
 
     def mixer(layer, mixed, hist):
@@ -215,18 +235,23 @@
         y_rows = (mixed[1] * long_two).astype(jnp.bfloat16)
         send_sum(2 * layer, jnp.dot(y_rows, wout[layer], preferred_element_type=jnp.float32))
         for g in range(3):
-            xb[layer, core, 2 * g:2 * g + 2, :] = prow[layer, g, STEPS:STEPS + 2, :]
-        xb[layer, core, 6:8, :] = jnp.zeros((2, chan), jnp.float32)
-        xb[layer, core, 8:8 + STEPS, :] = value
-        xb[layer, core, 8 + STEPS:8 + 2 * STEPS, :] = z_rows
-        swap_copy(layer).start()
+            xb[layer, own, 2 * g:2 * g + 2, :] = prow[layer, g, STEPS:STEPS + 2, :]
+        xb[layer, own, 6:8, :] = jnp.zeros((2, chan), jnp.float32)
+        xb[layer, own, 8:8 + STEPS, :] = value
+        xb[layer, own, 8 + STEPS:8 + 2 * STEPS, :] = z_rows
+        for copy in row_copies(layer, own):
+            copy.start()
 
     def mlp(layer, hidden):
         up = jnp.dot(layer_norm(hidden).astype(jnp.bfloat16), wup[layer], preferred_element_type=jnp.float32)
         return jnp.dot(jax.nn.gelu(up).astype(jnp.bfloat16), wdown[layer], preferred_element_type=jnp.float32)
 
     def put_rows(layer):
-        swap_copy(layer).wait_recv()
+        for b in range(SEQ):
+            @pl.when(sp != 2 * b + 1)
+            def _():
+                row_copy(layer, b, 0).wait_recv()
+
         for b in range(SEQ):
             newrow[2 * STEPS * b:2 * STEPS * (b + 1), 0:chan] = xb[layer, b, 8:16, :]
             for g in range(3):
@@ -241,54 +266,87 @@
                     moved = turned if at == 0 else pltpu.roll(turned, LANES - at, 1)
                     cache[layer, b, :, 0:LANES] = jnp.where(lane_c < STEPS, moved, 0.0).astype(jnp.bfloat16)
 
-    conv(0, 0, CHUNKS)
-    pl.semaphore_wait(barrier, 6)
-    send_hist(0)
     newrow[...] = jnp.zeros_like(newrow)
     rrow[...] = jnp.zeros_like(rrow)
+    conv(0, 0, CHUNKS)
+
+    @pl.when(carries)
+    def _():
+        pl.semaphore_wait(barrier, 6)
+
+    @pl.when(jnp.logical_not(carries))
+    def _():
+        pl.semaphore_wait(barrier, 3)
+
+    send_hist(0)
     for copy in smalls:
         copy.wait()
-    hidden = jnp.where(core == 0, jnp.concatenate([e_ref[j].astype(jnp.float32)[0:1] for j in range(STEPS)], axis=0),
-                       jnp.concatenate([e_ref[j].astype(jnp.float32)[1:2] for j in range(STEPS)], axis=0))
-    lag = [[jnp.transpose(lag_ref[layer, which])[:8] for which in range(2)] for layer in range(LAYERS)]
-    weight_copy(0, 0).wait()
-    mixed = project(0, hidden)
-    weight_copy(0, 1).wait()
-    mixer(0, mixed, sum_hist(0))
-    conv(1, 0, SPLIT)
-    weight_copy(0, 2).wait()
-    weight_copy(0, 3).wait()
-    hidden = hidden + take_sum(0) + bout_ref[0:1]
-    send_sum(1, mlp(0, hidden))
-    conv(1, SPLIT, CHUNKS)
-    send_hist(1)
-    weight_copy(1, 0).wait()
-    hidden = hidden + take_sum(1)
-    mixed = project(1, hidden)
-    weight_copy(1, 1).wait()
-    mixer(1, mixed, sum_hist(1))
-    put_rows(0)
-    weight_copy(1, 2).wait()
-    weight_copy(1, 3).wait()
-    hidden = hidden + take_sum(2) + bout_ref[1:2]
-    send_sum(3, mlp(1, hidden))
-    put_rows(1)
-    hidden = hidden + take_sum(3)
-    fin[core] = hidden
-    last = pltpu.make_async_remote_copy(fin.at[core], fin.at[core], fsem.at[0], fsem.at[1], device_id=partner, device_id_type=MESH)
-    last.start()
+
+    @pl.when(carries)
+    def _():
+        hidden = jnp.where(own == 0, jnp.concatenate([e_ref[j].astype(jnp.float32)[0:1] for j in range(STEPS)], axis=0),
+                           jnp.concatenate([e_ref[j].astype(jnp.float32)[1:2] for j in range(STEPS)], axis=0))
+        for layer in range(LAYERS):
+            for which in range(2):
+                lag[layer, which] = jnp.transpose(lag_ref[layer, which])[:8]
+        weight_copy(0, 0).wait()
+        mixed = project(0, hidden)
+        weight_copy(0, 1).wait()
+        mixer(0, mixed, sum_hist(0))
+        conv(1, 0, SPLIT)
+        weight_copy(0, 2).wait()
+        weight_copy(0, 3).wait()
+        hidden = hidden + take_sum(0) + bout_ref[0:1]
+        send_sum(1, mlp(0, hidden))
+        conv(1, SPLIT, CHUNKS)
+        send_hist(1)
+        weight_copy(1, 0).wait()
+        hidden = hidden + take_sum(1)
+        mixed = project(1, hidden)
+        weight_copy(1, 1).wait()
+        mixer(1, mixed, sum_hist(1))
+        put_rows(0)
+        weight_copy(1, 2).wait()
+        weight_copy(1, 3).wait()
+        hidden = hidden + take_sum(2) + bout_ref[1:2]
+        send_sum(3, mlp(1, hidden))
+        put_rows(1)
+        fin[own] = hidden + take_sum(3)
+        for copy in last_copies(own):
+            copy.start()
+        for layer in range(LAYERS):
+            for copy in row_copies(layer, own):
+                copy.wait_send()
+        for n in range(4):
+            for copy in sum_copies(n):
+                copy.wait_send()
+        for copy in last_copies(own):
+            copy.wait_send()
+
+    @pl.when(jnp.logical_not(carries))
+    def _():
+        conv(1, 0, CHUNKS)
+        send_hist(1)
+        for layer in range(LAYERS):
+            for n in range(4):
+                weight_copy(layer, n).wait()
+        put_rows(0)
+        put_rows(1)
+
     for layer in range(LAYERS):
-        swap_copy(layer).wait_send()
-
-        @pl.when(sp != 3)
+        @pl.when(has_rows)
         def _():
-            for copy in hist_copies(layer):
-                copy.wait_send()
-    for n in range(4):
-        for copy in sum_copies(n):
-            copy.wait_send()
-    last.wait()
+            hist_copy(layer, 1).wait_send()
+
+            @pl.when(sp != 1)
+            def _():
+                hist_copy(layer, 0).wait_send()
+
     for b in range(SEQ):
+        @pl.when(sp != 2 * b + 1)
+        def _():
+            last_copy(b, 0).wait_recv()
+
         for j in range(STEPS):
             hid_out[j, b:b + 1, :] = fin[b, j:j + 1, :]
 
@@ -353,6 +411,8 @@
                 pltpu.VMEM(w_up.shape, bf16),
                 pltpu.VMEM(w_down.shape, bf16),
                 pltpu.VMEM((2, chan, ROWS * LANES), f32),
+                pltpu.VMEM((chan, LANES), f32),
+                pltpu.VMEM((LAYERS, 2, 8, chan), f32),
                 pltpu.VMEM((LAYERS, 3, 8, chan), f32),
                 pltpu.VMEM((LAYERS, 2, 8, chan), f32),
                 pltpu.VMEM((LANES, 2 * LANES), f32),
@@ -363,12 +423,14 @@
                 dma((7,)),
                 dma((LAYERS, CHUNKS, 3)),
                 dma((LAYERS, 4)),
-                dma((LAYERS, 3)),
+                dma((LAYERS, SEQ)),
                 dma((LAYERS, 4)),
                 dma((4, 3)),
                 dma((4, 4)),
-                dma((LAYERS, 2)),
-                dma((2,)),
+                dma((LAYERS, 3)),
+                dma((LAYERS, SEQ)),
+                dma((3,)),
+                dma((SEQ,)),
             ],
             compiler_params=pltpu.CompilerParams(collective_id=0, has_side_effects=True, vmem_limit_bytes=40 * 1024 * 1024),
             name="decode",

time: 40.8 us -> 39.4 us (0.966)
  Pallas kernels: 40 us -> 38.6 us
    pallas_call x1, Pallas kernels: 35.4 us -> 33.9 us  [device_fn(): pl.pallas_call(kernel, out_shape=(jax.ShapeDtypeStruct(step_emb.shape, f3...]
where the time goes in v3:
time: 39.4 us; the launch traced here: 39.2 us
  Pallas kernels  38.6 us (98%)
  between operations  0.64 us (2%)
    pallas_call x1, Pallas kernels, device_fn(): pl.pallas_call(kernel, out_shape=(jax.ShapeDtypeStruct(step_emb.shape, f3...  33.9 us
    pallas_call x1, Pallas kernels, device_fn(): pl.pallas_call(emit, out_shape=(jax.ShapeDtypeStruct(hid.shape, f32), jax...  4.68 us

profile of v3, /device:TPU:0, one launch (start us, length us, event | category | flops | bytes accessed | tf_op | source)
XLA Modules:
  0.0 39.2 jit_solution(16371177252351310860)
XLA Ops:
  0.6 33.9 %decode.1 = (f32[4,2,768]{2,1,0:T(2,128)S(1)}, bf16[2,2,192,4096]{3,2,1,0:T(8,128)(2,1)S(1)}, bf16[2,2,192,4096]{3,2,1,0:T(8,128)(2,1)S(1)}, bf16[2,2,3,2,192]{4,3,2,1,0:T(2,128)(2,1)S(1)}) custom-call(bf16[4,2,768]{2,1,0:T(2,128)(2,1)} %e_hbm.1, bf16[2,2,192,4096]{3,2,1,0:T(8,128)(2,1)} %bitcast.11, bf16[2,2,192,4096]{3,2,1,0:T(8,128)(2,1)} %bitcast.12, ...), custom_call_target="tpu_custom_call" | custom-call | tf_op jit(solution)/shard_map/decode/pallas_call | solution.py:390
  34.5 4.7 %emit.1 = (f32[4,2,768]{2,1,0:T(2,128)}, bf16[2,2,192,4096]{3,2,1,0:T(8,128)(2,1)}, bf16[2,2,192,4096]{3,2,1,0:T(8,128)(2,1)}, bf16[2,2,3,2,192]{4,3,2,1,0:T(2,128)(2,1)}) custom-call(f32[4,2,768]{2,1,0:T(2,128)S(1)} %get-tuple-element.12.hid, bf16[2,2,192,4096]{3,2,1,0:T(8,128)(2,1)S(1)} %get-tuple-element.13.v, ...), custom_call_target="tpu_custom_call" | custom-call | tf_op jit(solution)/shard_map/emit/pallas_call | solution.py:438

commit v4 on v3

--- a/solution.py
+++ b/solution.py
@@ -13,7 +13,7 @@
 ROWS = STEPS * SEQ
 LANES = 128
 CHUNKS = 12
-SPLIT = 7
+SPLIT = 4
 MESH = pl.DeviceIdType.MESH
 
 
@@ -27,7 +27,7 @@
 def kernel(e_hbm, v_hbm, z_hbm, st_hbm, win_hbm, bin_hbm, tap_hbm, h_hbm, skip_hbm, wout_hbm, bout_hbm, wup_hbm, wdown_hbm,
            hid_out, v_ref, z_ref, st_out,
            e_ref, st_ref, win, bin_ref, tap_ref, h_ref, lag_ref, skip_ref, wout, bout_ref, wup, wdown,
-           acc, total, lag, prow, rrow, newrow, hx, ar, xb, fin,
+           flip, v_even, z_even, v_odd, z_odd, acc, total, lag, prow, rrow, newrow, hx, ar, xb, fin, held,
            small_sem, chunk_sem, w_sem, hsend, hrecv, asend, arecv, xsend, xrecv, fsend, frecv):
     tp = lax.axis_index("tp")
     sp = lax.axis_index("sp")
@@ -70,60 +70,56 @@
         src, dst = ((win_hbm, win), (wout_hbm, wout), (wup_hbm, wup), (wdown_hbm, wdown))[n]
         return pltpu.make_async_copy(src.at[layer], dst.at[layer], w_sem.at[layer, n])
 
-    for layer in range(LAYERS):
-        for k in range(CHUNKS):
-            for copy in chunk_copies(layer, k):
-                copy.start()
-        if layer == 0:
+    def start_weights(layer):
+        @pl.when(carries)
+        def _():
+            for n in range(4):
+                weight_copy(layer, n).start()
+
+    for n in range(LAYERS * CHUNKS):
+        layer, k = divmod(n, CHUNKS)
+        for copy in chunk_copies(layer, k):
+            copy.start()
+        if n == CHUNKS:
             for copy in smalls:
                 copy.start()
-        for n in range(4):
-            weight_copy(layer, n).start()
+            start_weights(0)
+    start_weights(1)
 
     lane8 = lax.broadcasted_iota(jnp.int32, (8, LANES), 1)
     lane16 = lax.broadcasted_iota(jnp.int32, (16, LANES), 1)
-    flip = [lax.rem(a - lane8 + 2 * LANES, LANES) for a in range(2)]
-
-    def conv_group(cache, layer, which, row):
-        accs = [[[None] * SEQ for _ in range(STEPS)] for _ in range(2)]
-
-        def flipped(u, t):
-            x = h_ref[layer, which, pl.ds(row + 8 * u, 8), LANES * t:LANES * (t + 1)]
-            return [jnp.take_along_axis(x, flip[a], axis=1) for a in range(2)]
+    spans = range(-1, tiles)
+
+    def turn(cache, layer, row, dst):
+        zero = jnp.zeros((16, LANES), jnp.bfloat16)
 
         def values(b, m):
-            return cache[layer, b, pl.ds(row, 16), LANES * m:LANES * (m + 1)]
-
-        zero = jnp.zeros((16, LANES), jnp.bfloat16)
-        cur = [flipped(u, tiles) for u in range(2)]
-        val = [values(b, 0) for b in range(SEQ)]
-        rot = [pltpu.roll(val[b], LANES - 2, 1) for b in range(SEQ)]
-        for b in range(SEQ):
-            edge = jnp.where(lane16 >= LANES - 2, rot[b], zero).astype(jnp.float32)
-            for u in range(2):
-                for a in range(2):
-                    accs[u][a + 2][b] = cur[u][a] * edge[8 * u:8 * u + 8]
-        for m in range(tiles):
-            nxt = [flipped(u, tiles - 1 - m) for u in range(2)]
-            last = m == tiles - 1
-            val_n = [None if last else values(b, m + 1) for b in range(SEQ)]
-            rot_n = [zero if last else pltpu.roll(val_n[b], LANES - 2, 1) for b in range(SEQ)]
-            here = [val[b].astype(jnp.float32) for b in range(SEQ)]
-            ahead = [jnp.where(lane16 < LANES - 2, rot[b], rot_n[b]).astype(jnp.float32) for b in range(SEQ)]
-            for u in range(2):
-                for a in range(2):
-                    taps = jnp.where(lane8 <= a, cur[u][a], nxt[u][a])
-                    for b in range(SEQ):
-                        p0 = taps * here[b][8 * u:8 * u + 8]
-                        p2 = taps * ahead[b][8 * u:8 * u + 8]
-                        accs[u][a][b] = p0 if m == 0 else accs[u][a][b] + p0
-                        accs[u][a + 2][b] = accs[u][a + 2][b] + p2
-            cur, val, rot = nxt, val_n, rot_n
+            return cache[layer, b, pl.ds(row, 16), LANES * m:LANES * (m + 1)] if 0 <= m < tiles else zero
+
+        parts = [jnp.concatenate([values(b, m), values(b, m + 1)], axis=1) for m in spans for b in range(SEQ)]
+        dst[...] = jnp.dot(jnp.concatenate(parts, axis=0), flip[...], preferred_element_type=jnp.float32)
+
+    def gather(layer, which, row, src):
         for u in range(2):
+            accs = [[None] * SEQ for _ in range(STEPS)]
+            after = None
+            for m in spans:
+                even = h_ref[layer, which, pl.ds(row + 8 * u, 8), LANES * (tiles - 1 - m):LANES * (tiles - m)]
+                rolled = pltpu.roll(even, LANES - 1, 1)
+                odd = rolled if after is None else jnp.where(lane8 < LANES - 1, rolled, after)
+                after = rolled
+                for b in range(SEQ):
+                    base = 16 * (SEQ * (m + 1) + b) + 8 * u
+                    for two in range(2):
+                        value = src[base:base + 8, LANES * two:LANES * (two + 1)]
+                        for one, taps in enumerate((even, odd)):
+                            part = taps * value
+                            j = 2 * two + one
+                            accs[j][b] = part if accs[j][b] is None else accs[j][b] + part
             for j in range(STEPS):
                 for b in range(SEQ):
                     n = SEQ * j + b
-                    acc[which, pl.ds(row + 8 * u, 8), LANES * n:LANES * (n + 1)] = accs[u][j][b]
+                    acc[which, pl.ds(row + 8 * u, 8), LANES * n:LANES * (n + 1)] = accs[j][b]
 
     def close(row):
         out = jnp.zeros((16, LANES), jnp.float32)
@@ -135,20 +131,37 @@
                     out = jnp.where(lane16 == (2 * b + which) * STEPS + j, part, out)
         total[pl.ds(row, 16), :] = out
 
-    def conv(layer, k0, k1):
-        def chunk(k, _):
-            for copy in chunk_copies(layer, k):
+    def row_of(k):
+        return k * 16 if isinstance(k, int) else pl.multiple_of(k * 16, 16)
+
+    def conv(layer, p0, p1):
+        def pair(p, _):
+            k = 2 * p
+            step = layer * CHUNKS + k + 2
+            later, after = lax.rem(lax.div(step, CHUNKS), LAYERS), lax.rem(step, CHUNKS)
+            for copy in chunk_copies(layer, k + 1):
                 copy.wait()
+
+            @pl.when(step < LAYERS * CHUNKS)
+            def _():
+                for copy in chunk_copies(later, after):
+                    copy.wait()
 
             @pl.when(has_rows)
             def _():
-                row = pl.multiple_of(k * 16, 16)
-                conv_group(v_ref, layer, 0, row)
-                conv_group(z_ref, layer, 1, row)
+                r0, r1, r2 = row_of(k), row_of(k + 1), row_of(after)
+                turn(v_ref, layer, r1, v_odd)
+                gather(layer, 0, r0, v_even)
+                turn(z_ref, layer, r1, z_odd)
+                gather(layer, 1, r0, z_even)
+                turn(v_ref, later, r2, v_even)
+                gather(layer, 0, r1, v_odd)
+                turn(z_ref, later, r2, z_even)
+                gather(layer, 1, r1, z_odd)
 
             return 0
 
-        lax.fori_loop(k0, k1, chunk, 0)
+        lax.fori_loop(p0, p1, pair, 0)
 
     lane_c = lax.broadcasted_iota(jnp.int32, (chan, LANES), 1)
 
@@ -157,18 +170,16 @@
                                             device_id={"sp": 2 * seq + 1}, device_id_type=MESH)
 
     def send_hist(layer):
-        @pl.when(has_rows)
-        def _():
-            for row in range(0, chan, 16):
-                close(row)
-            turned = jnp.transpose(total[...])
-            for b in range(SEQ):
-                hx[layer, sp, b] = turned[2 * STEPS * b:2 * STEPS * (b + 1)]
-            hist_copy(layer, 1).start()
-
-            @pl.when(sp != 1)
-            def _():
-                hist_copy(layer, 0).start()
+        for row in range(0, chan, 16):
+            close(row)
+        turned = jnp.transpose(total[...])
+        for b in range(SEQ):
+            hx[layer, sp, b] = turned[2 * STEPS * b:2 * STEPS * (b + 1)]
+        hist_copy(layer, 1).start()
+
+        @pl.when(sp != 1)
+        def _():
+            hist_copy(layer, 0).start()
 
     def sum_hist(layer):
         for src in range(3):
@@ -268,40 +279,66 @@
 
     newrow[...] = jnp.zeros_like(newrow)
     rrow[...] = jnp.zeros_like(rrow)
-    conv(0, 0, CHUNKS)
+    kk = lax.broadcasted_iota(jnp.int32, flip.shape, 0)
+    nn = lax.broadcasted_iota(jnp.int32, flip.shape, 1)
+    flip[...] = jnp.where(kk == jnp.where(nn < LANES, LANES - nn, 2 * LANES + 2 - nn), 1.0, 0.0).astype(jnp.bfloat16)
+    for copy in chunk_copies(0, 0):
+        copy.wait()
+
+    @pl.when(has_rows)
+    def _():
+        turn(v_ref, 0, 0, v_even)
+        turn(z_ref, 0, 0, z_even)
+
+    def stage(n, _):
+        conv(lax.div(n + 1, 2), SPLIT * lax.div(n, 2), CHUNKS // 2 - (CHUNKS // 2 - SPLIT) * lax.rem(n, 2))
+
+        @pl.when((n == 0) & carries)
+        def _():
+            pl.semaphore_wait(barrier, 6)
+
+        @pl.when((n == 0) & jnp.logical_not(carries))
+        def _():
+            pl.semaphore_wait(barrier, 3)
+
+        @pl.when((n != 1) & has_rows)
+        def _():
+            send_hist(lax.div(n, 2))
+
+        @pl.when(n == 0)
+        def _():
+            for copy in smalls:
+                copy.wait()
+
+        @pl.when((n == 0) & carries)
+        def _():
+            hidden = jnp.where(own == 0, jnp.concatenate([e_ref[j].astype(jnp.float32)[0:1] for j in range(STEPS)], axis=0),
+                               jnp.concatenate([e_ref[j].astype(jnp.float32)[1:2] for j in range(STEPS)], axis=0))
+            for layer in range(LAYERS):
+                for which in range(2):
+                    lag[layer, which] = jnp.transpose(lag_ref[layer, which])[:8]
+            weight_copy(0, 0).wait()
+            mixed = project(0, hidden)
+            weight_copy(0, 1).wait()
+            mixer(0, mixed, sum_hist(0))
+            held[...] = hidden
+
+        @pl.when((n == 1) & carries)
+        def _():
+            weight_copy(0, 2).wait()
+            weight_copy(0, 3).wait()
+            hidden = held[...] + take_sum(0) + bout_ref[0:1]
+            send_sum(1, mlp(0, hidden))
+            held[...] = hidden
+
+        return 0
+
+    lax.fori_loop(0, 3, stage, 0)
 
     @pl.when(carries)
     def _():
-        pl.semaphore_wait(barrier, 6)
-
-    @pl.when(jnp.logical_not(carries))
-    def _():
-        pl.semaphore_wait(barrier, 3)
-
-    send_hist(0)
-    for copy in smalls:
-        copy.wait()
-
-    @pl.when(carries)
-    def _():
-        hidden = jnp.where(own == 0, jnp.concatenate([e_ref[j].astype(jnp.float32)[0:1] for j in range(STEPS)], axis=0),
-                           jnp.concatenate([e_ref[j].astype(jnp.float32)[1:2] for j in range(STEPS)], axis=0))
-        for layer in range(LAYERS):
-            for which in range(2):
-                lag[layer, which] = jnp.transpose(lag_ref[layer, which])[:8]
-        weight_copy(0, 0).wait()
-        mixed = project(0, hidden)
-        weight_copy(0, 1).wait()
-        mixer(0, mixed, sum_hist(0))
-        conv(1, 0, SPLIT)
-        weight_copy(0, 2).wait()
-        weight_copy(0, 3).wait()
-        hidden = hidden + take_sum(0) + bout_ref[0:1]
-        send_sum(1, mlp(0, hidden))
-        conv(1, SPLIT, CHUNKS)
-        send_hist(1)
         weight_copy(1, 0).wait()
-        hidden = hidden + take_sum(1)
+        hidden = held[...] + take_sum(1)
         mixed = project(1, hidden)
         weight_copy(1, 1).wait()
         mixer(1, mixed, sum_hist(1))
@@ -325,11 +362,6 @@
 
     @pl.when(jnp.logical_not(carries))
     def _():
-        conv(1, 0, CHUNKS)
-        send_hist(1)
-        for layer in range(LAYERS):
-            for n in range(4):
-                weight_copy(layer, n).wait()
         put_rows(0)
         put_rows(1)
 
@@ -410,6 +442,8 @@
                 pltpu.VMEM(b_out.shape, f32),
                 pltpu.VMEM(w_up.shape, bf16),
                 pltpu.VMEM(w_down.shape, bf16),
+                pltpu.VMEM((2 * LANES, 2 * LANES), bf16),
+                *[pltpu.VMEM((16 * SEQ * (shard_len // LANES + 1), 2 * LANES), f32)] * 4,
                 pltpu.VMEM((2, chan, ROWS * LANES), f32),
                 pltpu.VMEM((chan, LANES), f32),
                 pltpu.VMEM((LAYERS, 2, 8, chan), f32),
@@ -420,6 +454,7 @@
                 pltpu.VMEM((4, 4, STEPS, model), f32),
                 pltpu.VMEM((LAYERS, SEQ, 16, chan), f32),
                 pltpu.VMEM((SEQ, STEPS, model), f32),
+                pltpu.VMEM((STEPS, model), f32),
                 dma((7,)),
                 dma((LAYERS, CHUNKS, 3)),
                 dma((LAYERS, 4)),

time: 39.4 us -> 38.9 us (0.987)
  Pallas kernels: 38.6 us -> 38.1 us
    pallas_call x1, Pallas kernels: 33.9 us -> 33.4 us  [device_fn(): pl.pallas_call(kernel, out_shape=(jax.ShapeDtypeStruct(step_emb.shape, f3...]
where the time goes in v4:
time: 38.9 us; the launch traced here: 38.7 us
  Pallas kernels  38.1 us (98%)
  between operations  0.64 us (2%)
    pallas_call x1, Pallas kernels, device_fn(): pl.pallas_call(kernel, out_shape=(jax.ShapeDtypeStruct(step_emb.shape, f3...  33.4 us
    pallas_call x1, Pallas kernels, device_fn(): pl.pallas_call(emit, out_shape=(jax.ShapeDtypeStruct(hid.shape, f32), jax...  4.68 us

profile of v4, /device:TPU:0, one launch (start us, length us, event | category | flops | bytes accessed | tf_op | source)
XLA Modules:
  0.0 38.7 jit_solution(10927343777410957738)
XLA Ops:
  0.6 33.4 %decode.1 = (f32[4,2,768]{2,1,0:T(2,128)S(1)}, bf16[2,2,192,4096]{3,2,1,0:T(8,128)(2,1)S(1)}, bf16[2,2,192,4096]{3,2,1,0:T(8,128)(2,1)S(1)}, bf16[2,2,3,2,192]{4,3,2,1,0:T(2,128)(2,1)S(1)}) custom-call(bf16[4,2,768]{2,1,0:T(2,128)(2,1)} %e_hbm.1, bf16[2,2,192,4096]{3,2,1,0:T(8,128)(2,1)} %bitcast.11, bf16[2,2,192,4096]{3,2,1,0:T(8,128)(2,1)} %bitcast.12, ...), custom_call_target="tpu_custom_call" | custom-call | tf_op jit(solution)/shard_map/decode/pallas_call | solution.py:422
  34.0 4.7 %emit.1 = (f32[4,2,768]{2,1,0:T(2,128)}, bf16[2,2,192,4096]{3,2,1,0:T(8,128)(2,1)}, bf16[2,2,192,4096]{3,2,1,0:T(8,128)(2,1)}, bf16[2,2,3,2,192]{4,3,2,1,0:T(2,128)(2,1)}) custom-call(f32[4,2,768]{2,1,0:T(2,128)S(1)} %get-tuple-element.12.hid, bf16[2,2,192,4096]{3,2,1,0:T(8,128)(2,1)S(1)} %get-tuple-element.13.v, ...), custom_call_target="tpu_custom_call" | custom-call | tf_op jit(solution)/shard_map/emit/pallas_call | solution.py:473

commit v5 on v4

--- a/solution.py
+++ b/solution.py
@@ -13,7 +13,7 @@
 ROWS = STEPS * SEQ
 LANES = 128
 CHUNKS = 12
-SPLIT = 4
+FIRST, SECOND = 2, 3
 MESH = pl.DeviceIdType.MESH
 
 
@@ -27,7 +27,7 @@
 def kernel(e_hbm, v_hbm, z_hbm, st_hbm, win_hbm, bin_hbm, tap_hbm, h_hbm, skip_hbm, wout_hbm, bout_hbm, wup_hbm, wdown_hbm,
            hid_out, v_ref, z_ref, st_out,
            e_ref, st_ref, win, bin_ref, tap_ref, h_ref, lag_ref, skip_ref, wout, bout_ref, wup, wdown,
-           flip, v_even, z_even, v_odd, z_odd, acc, total, lag, prow, rrow, newrow, hx, ar, xb, fin, held,
+           flip, v_even, z_even, v_odd, z_odd, acc, total, lag, prow, rrow, newrow, hx, ar, xb, fin, held, mixed_ref,
            small_sem, chunk_sem, w_sem, hsend, hrecv, asend, arecv, xsend, xrecv, fsend, frecv):
     tp = lax.axis_index("tp")
     sp = lax.axis_index("sp")
@@ -291,7 +291,10 @@
         turn(z_ref, 0, 0, z_even)
 
     def stage(n, _):
-        conv(lax.div(n + 1, 2), SPLIT * lax.div(n, 2), CHUNKS // 2 - (CHUNKS // 2 - SPLIT) * lax.rem(n, 2))
+        at_least = [None] + [lax.div(n + 3 - i, 3) if i == 1 else lax.div(n, i) for i in (1, 2, 3)]
+        conv(at_least[1], FIRST * at_least[2] + SECOND * at_least[3],
+             CHUNKS // 2 - (CHUNKS // 2 - FIRST) * (at_least[1] - at_least[2])
+             - (CHUNKS // 2 - FIRST - SECOND) * (at_least[2] - at_least[3]))
 
         @pl.when((n == 0) & carries)
         def _():
@@ -301,9 +304,9 @@
         def _():
             pl.semaphore_wait(barrier, 3)
 
-        @pl.when((n != 1) & has_rows)
-        def _():
-            send_hist(lax.div(n, 2))
+        @pl.when(((n == 0) | (n == 3)) & has_rows)
+        def _():
+            send_hist(lax.div(n, 3))
 
         @pl.when(n == 0)
         def _():
@@ -314,26 +317,29 @@
         def _():
             hidden = jnp.where(own == 0, jnp.concatenate([e_ref[j].astype(jnp.float32)[0:1] for j in range(STEPS)], axis=0),
                                jnp.concatenate([e_ref[j].astype(jnp.float32)[1:2] for j in range(STEPS)], axis=0))
+            held[...] = hidden
+            weight_copy(0, 0).wait()
+            for g, rows_f in enumerate(project(0, hidden)):
+                mixed_ref[g] = rows_f
             for layer in range(LAYERS):
                 for which in range(2):
                     lag[layer, which] = jnp.transpose(lag_ref[layer, which])[:8]
-            weight_copy(0, 0).wait()
-            mixed = project(0, hidden)
-            weight_copy(0, 1).wait()
-            mixer(0, mixed, sum_hist(0))
-            held[...] = hidden
+            for n_w in (1, 2, 3):
+                weight_copy(0, n_w).wait()
 
         @pl.when((n == 1) & carries)
         def _():
-            weight_copy(0, 2).wait()
-            weight_copy(0, 3).wait()
+            mixer(0, [mixed_ref[g] for g in range(3)], sum_hist(0))
+
+        @pl.when((n == 2) & carries)
+        def _():
             hidden = held[...] + take_sum(0) + bout_ref[0:1]
             send_sum(1, mlp(0, hidden))
             held[...] = hidden
 
         return 0
 
-    lax.fori_loop(0, 3, stage, 0)
+    lax.fori_loop(0, 4, stage, 0)
 
     @pl.when(carries)
     def _():
@@ -455,6 +461,7 @@
                 pltpu.VMEM((LAYERS, SEQ, 16, chan), f32),
                 pltpu.VMEM((SEQ, STEPS, model), f32),
                 pltpu.VMEM((STEPS, model), f32),
+                pltpu.VMEM((3, STEPS, chan), f32),
                 dma((7,)),
                 dma((LAYERS, CHUNKS, 3)),
                 dma((LAYERS, 4)),

time: 38.9 us -> 37.2 us (0.956)
  Pallas kernels: 38.1 us -> 36.4 us
    pallas_call x1, Pallas kernels: 33.4 us -> 31.8 us  [device_fn(): pl.pallas_call(kernel, out_shape=(jax.ShapeDtypeStruct(step_emb.shape, f3...]
where the time goes in v5:
time: 37.2 us; the launch traced here: 37.1 us
  Pallas kernels  36.4 us (98%)
  between operations  0.64 us (2%)
    pallas_call x1, Pallas kernels, device_fn(): pl.pallas_call(kernel, out_shape=(jax.ShapeDtypeStruct(step_emb.shape, f3...  31.8 us
    pallas_call x1, Pallas kernels, device_fn(): pl.pallas_call(emit, out_shape=(jax.ShapeDtypeStruct(hid.shape, f32), jax...  4.68 us

profile of v5, /device:TPU:0, one launch (start us, length us, event | category | flops | bytes accessed | tf_op | source)
XLA Modules:
  0.0 37.1 jit_solution(3149574623563469625)
XLA Ops:
  0.6 31.8 %decode.1 = (f32[4,2,768]{2,1,0:T(2,128)S(1)}, bf16[2,2,192,4096]{3,2,1,0:T(8,128)(2,1)S(1)}, bf16[2,2,192,4096]{3,2,1,0:T(8,128)(2,1)S(1)}, bf16[2,2,3,2,192]{4,3,2,1,0:T(2,128)(2,1)S(1)}) custom-call(bf16[4,2,768]{2,1,0:T(2,128)(2,1)} %e_hbm.1, bf16[2,2,192,4096]{3,2,1,0:T(8,128)(2,1)} %bitcast.11, bf16[2,2,192,4096]{3,2,1,0:T(8,128)(2,1)} %bitcast.12, ...), custom_call_target="tpu_custom_call" | custom-call | tf_op jit(solution)/shard_map/decode/pallas_call | solution.py:428
  32.4 4.7 %emit.1 = (f32[4,2,768]{2,1,0:T(2,128)}, bf16[2,2,192,4096]{3,2,1,0:T(8,128)(2,1)}, bf16[2,2,192,4096]{3,2,1,0:T(8,128)(2,1)}, bf16[2,2,3,2,192]{4,3,2,1,0:T(2,128)(2,1)}) custom-call(f32[4,2,768]{2,1,0:T(2,128)S(1)} %get-tuple-element.12.hid, bf16[2,2,192,4096]{3,2,1,0:T(8,128)(2,1)S(1)} %get-tuple-element.13.v, ...), custom_call_target="tpu_custom_call" | custom-call | tf_op jit(solution)/shard_map/emit/pallas_call | solution.py:480

commit v6 on v5

--- a/solution.py
+++ b/solution.py
@@ -14,6 +14,7 @@
 LANES = 128
 CHUNKS = 12
 FIRST, SECOND = 2, 3
+AHEAD = 6
 MESH = pl.DeviceIdType.MESH
 
 
@@ -76,15 +77,31 @@
             for n in range(4):
                 weight_copy(layer, n).start()
 
-    for n in range(LAYERS * CHUNKS):
-        layer, k = divmod(n, CHUNKS)
-        for copy in chunk_copies(layer, k):
+    for k in range(AHEAD):
+        for copy in chunk_copies(0, k):
             copy.start()
-        if n == CHUNKS:
+
+    def start_ahead(layer, p):
+        for n in range(2):
+            step = layer * CHUNKS + 2 * p + AHEAD + n
+
+            @pl.when(step < LAYERS * CHUNKS)
+            def _():
+                for copy in chunk_copies(lax.div(step, CHUNKS), lax.rem(step, CHUNKS)):
+                    copy.start()
+
+        @pl.when((layer == 0) & (p == 1))
+        def _():
             for copy in smalls:
                 copy.start()
+
+        @pl.when((layer == 0) & (p == 2))
+        def _():
             start_weights(0)
-    start_weights(1)
+
+        @pl.when((layer == 1) & (p == 1))
+        def _():
+            start_weights(1)
 
     lane8 = lax.broadcasted_iota(jnp.int32, (8, LANES), 1)
     lane16 = lax.broadcasted_iota(jnp.int32, (16, LANES), 1)
@@ -139,6 +156,7 @@
             k = 2 * p
             step = layer * CHUNKS + k + 2
             later, after = lax.rem(lax.div(step, CHUNKS), LAYERS), lax.rem(step, CHUNKS)
+            start_ahead(layer, p)
             for copy in chunk_copies(layer, k + 1):
                 copy.wait()
 
@@ -393,8 +411,10 @@
     copies = []
     for layer in range(LAYERS):
         for b in range(SEQ):
-            copies += [(v.at[layer, b], v_o.at[layer, b]), (z.at[layer, b], z_o.at[layer, b])]
-    copies += [(hid, hid_o), (st, st_o)]
+            for part in range(2):
+                rows = pl.ds(part * v.shape[2] // 2, v.shape[2] // 2)
+                copies += [(v.at[layer, b, rows], v_o.at[layer, b, rows]), (z.at[layer, b, rows], z_o.at[layer, b, rows])]
+    copies = [(hid, hid_o), (st, st_o)] + copies
     copies = [pltpu.make_async_copy(src, dst, sem.at[n]) for n, (src, dst) in enumerate(copies)]
     for copy in copies:
         copy.start()
@@ -487,7 +507,7 @@
             ),
             in_specs=[pl.BlockSpec(memory_space=pltpu.VMEM)] * 4,
             out_specs=[pl.BlockSpec(memory_space=pltpu.HBM)] * 4,
-            scratch_shapes=[dma((4 * LAYERS + 2,))],
+            scratch_shapes=[dma((8 * LAYERS + 2,))],
             compiler_params=pltpu.CompilerParams(vmem_limit_bytes=1024 * 1024),
             name="emit",
         )(hid, v_out, z_out, st_out)

time: 37.2 us -> 37.8 us (1.016)
  Pallas kernels: 36.4 us -> 37 us
    pallas_call x1, Pallas kernels: 31.8 us -> 32.3 us  [device_fn(): pl.pallas_call(kernel, out_shape=(jax.ShapeDtypeStruct(step_emb.shape, f3...]
where the time goes in v6:
time: 37.8 us; the launch traced here: 37.6 us
  Pallas kernels  37 us (98%)
  between operations  0.64 us (2%)
    pallas_call x1, Pallas kernels, device_fn(): pl.pallas_call(kernel, out_shape=(jax.ShapeDtypeStruct(step_emb.shape, f3...  32.3 us
    pallas_call x1, Pallas kernels, device_fn(): pl.pallas_call(emit, out_shape=(jax.ShapeDtypeStruct(hid.shape, f32), jax...  4.73 us

profile of v6, /device:TPU:0, one launch (start us, length us, event | category | flops | bytes accessed | tf_op | source)
XLA Modules:
  0.0 37.6 jit_solution(1664787030579783697)
XLA Ops:
  0.6 32.3 %decode.1 = (f32[4,2,768]{2,1,0:T(2,128)S(1)}, bf16[2,2,192,4096]{3,2,1,0:T(8,128)(2,1)S(1)}, bf16[2,2,192,4096]{3,2,1,0:T(8,128)(2,1)S(1)}, bf16[2,2,3,2,192]{4,3,2,1,0:T(2,128)(2,1)S(1)}) custom-call(bf16[4,2,768]{2,1,0:T(2,128)(2,1)} %e_hbm.1, bf16[2,2,192,4096]{3,2,1,0:T(8,128)(2,1)} %bitcast.11, bf16[2,2,192,4096]{3,2,1,0:T(8,128)(2,1)} %bitcast.12, ...), custom_call_target="tpu_custom_call" | custom-call | tf_op jit(solution)/shard_map/decode/pallas_call | solution.py:448
  32.9 4.7 %emit.1 = (f32[4,2,768]{2,1,0:T(2,128)}, bf16[2,2,192,4096]{3,2,1,0:T(8,128)(2,1)}, bf16[2,2,192,4096]{3,2,1,0:T(8,128)(2,1)}, bf16[2,2,3,2,192]{4,3,2,1,0:T(2,128)(2,1)}) custom-call(f32[4,2,768]{2,1,0:T(2,128)S(1)} %get-tuple-element.12.hid, bf16[2,2,192,4096]{3,2,1,0:T(8,128)(2,1)S(1)} %get-tuple-element.13.v, ...), custom_call_target="tpu_custom_call" | custom-call | tf_op jit(solution)/shard_map/emit/pallas_call | solution.py:500
